TPU v7x, 256 devices: a whole 4x4x8 slice. The times are simulated.
256 devices in a mesh: depth: 32 (over x, y, core), rays: 8 (over z).
Axes of the slice: x: 4, y: 4, z: 8, core: 2. Of those that a mesh axis runs over, the one named last changes fastest.
Arguments:
- density: float32 [1024, 131072], P('depth', 'rays'), may hold values from 4.8828125e-05 to 0.80390625
- radiance: float32 [3, 1024, 131072], P(None, 'depth', 'rays'), may hold values from 0 to 1
- target: float32 [3, 131072], P(None, 'rays'), may hold values from 0 to 1
Outputs:
- grad_density: float32 [1024, 131072], P('depth', 'rays')
- loss_mean: float32 [], replicated
All inputs are finite; a program needn't handle non-finite values.
Results may differ from a plain program's by a relative error of at most 0.0003.
Values sent between devices are 32-bit elements; how exact they have to be, the bound alone decides.
No kernel may reach another device: no remote copies, remote signals or barrier semaphores. Data moves between devices by JAX's collectives and lax.ppermute only.
A program may use at most 128 MiB of HBM per device.

v0:
```python
import jax
import jax.numpy as jnp
from jax import lax
from jax.sharding import PartitionSpec as P


def shifted(value, axis, steps):
    count = lax.axis_size(axis)
    initial, last = (max(0, -steps), min(count, count - steps))
    return lax.ppermute(value, axis, [(source, source + steps) for source in range(initial, last)])


def copy_for_each(shard, axis):
    size = lax.axis_size(axis)
    return lax.all_to_all(
        jnp.broadcast_to(shard[None], (size, *shard.shape)), axis, 0, 0, tiled=True
    )


def taken_together(shard, axis):
    return copy_for_each(shard, axis).sum(axis=0)


def on_device(density, radiance, target):
    sample_count = density.shape[0]
    ray_count = density.shape[1]
    rim_density, rim_color = shifted((density[:1], radiance[:, :1]), "depth", -1)
    sample_density = 0.5 * (density + jnp.concatenate([density[1:], rim_density], axis=0))
    sample_color = 0.5 * (radiance + jnp.concatenate([radiance[:, 1:], rim_color], axis=1))
    opacity = -jnp.expm1(-sample_density)
    zero_row = jnp.zeros((1, ray_count), jnp.float32)
    position = lax.broadcasted_iota(jnp.int32, (sample_count, sample_count), 0)
    vertical_element = lax.broadcasted_iota(jnp.int32, (sample_count, sample_count), 1)
    strict_ones = (position > vertical_element).astype(jnp.float32)
    lower_ones = (position >= vertical_element).astype(jnp.float32)
    optical = jnp.dot(strict_ones, sample_density, precision=lax.Precision.HIGHEST)
    slab_depth = optical[-1] + sample_density[-1]
    local_transmit = jnp.exp(-optical)
    emitted = (local_transmit * opacity)[None] * sample_color
    color_prefix = jnp.einsum("ij,cjr->cir", lower_ones, emitted, precision=lax.Precision.HIGHEST)
    slab_color = color_prefix[:, -1]
    stacked = jnp.concatenate([slab_depth[None], slab_color], axis=0)[None]
    all_slabs = lax.all_gather(stacked, "depth", axis=0, tiled=True)
    depths = all_slabs[:, 0]
    depth_running = jnp.cumsum(depths, axis=0)
    starts = jnp.concatenate([zero_row, depth_running[:-1]], axis=0)
    weighted = jnp.exp(-starts)[:, None, :] * all_slabs[:, 1:]
    slab_number = jnp.arange(all_slabs.shape[0], dtype=jnp.int32)
    earlier_mask = slab_number < lax.axis_index("depth")
    start_depth = jnp.sum(jnp.where(earlier_mask[:, None], depths, 0.0), axis=0)
    color_before = jnp.sum(jnp.where(earlier_mask[:, None, None], weighted, 0.0), axis=0)
    pixel_color = jnp.sum(weighted, axis=0)
    offset = jnp.exp(-start_depth)
    transmit = offset[None] * local_transmit
    remaining = (
        pixel_color[:, None, :] - color_before[:, None, :] - offset[None, None, :] * color_prefix
    )
    residual_grad = 2.0 * (pixel_color - target)
    transmit_next = transmit * jnp.exp(-sample_density)
    bracket = transmit_next[None] * sample_color - remaining
    sample_grad = jnp.sum(residual_grad[:, None, :] * bracket, axis=0)
    previous = shifted(sample_grad[-1:], "depth", 1)
    grad_density = 0.5 * (sample_grad + jnp.concatenate([previous, sample_grad[:-1]], axis=0))
    error_term = pixel_color - target
    loss_part = jnp.sum(error_term * error_term)
    total_rays = ray_count * lax.axis_size("rays")
    loss_mean = taken_together(loss_part, "rays") / (3.0 * total_rays)
    return (grad_density, loss_mean)


def solution(mesh):
    in_specs = (P("depth", "rays"), P(None, "depth", "rays"), P(None, "rays"))
    out_specs = (P("depth", "rays"), P())
    return jax.shard_map(
        on_device, mesh=mesh, in_specs=in_specs, out_specs=out_specs, check_vma=False
    )
```

profile of v0, /device:TPU:1, one launch (start us, length us, event | category | flops | bytes accessed | tf_op | source)
XLA Modules:
  0.0 155.6 jit_solution(2430280081989123533)
XLA Ops:
  7.2 1.1 slice.37
  8.3 5.1 %collective-permute-start = (f32[1,16384]{1,0:T(1,128)S(1)}, f32[1,16384]{1,0:T(1,128)S(1)}, u32[]{:S(2)}, u32[]{:S(2)}) collective-permute-start(f32[1,16384]{1,0:T(1,128)S(1)} %slice.37), channel_id=1, source_target_pairs={{8,0},{16,8},{24,16},{32,24},{40,32},{48,40},{56,48},{64,56},{72,6... | collective-permute-start | bytes 196616 | tf_op jit(solution)/shard_map/ppermute | solution.py:10
  13.4 1.5 slice.41
  14.9 1.9 %collective-permute-start.1 = (f32[3,1,16384]{2,1,0:T(1,128)S(1)}, f32[3,1,16384]{2,1,0:T(1,128)S(1)}, u32[]{:S(2)}, u32[]{:S(2)}) collective-permute-start(f32[3,1,16384]{2,1,0:T(1,128)S(1)} %slice.41), channel_id=1, source_target_pairs={{8,0},{16,8},{24,16},{32,24},{40,32},{48,40},{56,48},{64,56},{72,6... | collective-permute-start | bytes 589832 | tf_op jit(solution)/shard_map/ppermute | solution.py:10
  16.9 1.7 %slice.36 = f32[31,16384]{1,0:T(8,128)S(1)} slice(f32[32,16384]{1,0:T(8,128)} %param.3), slice={[1:32], [0:16384]} | slice | bytes 4063232 | tf_op jit(solution)/shard_map/slice | solution.py:28
  18.6 3.6 %slice.40 = f32[3,31,16384]{2,1,0:T(8,128)S(1)} slice(f32[3,32,16384]{2,1,0:T(8,128)} %param.4), slice={[0:3], [1:32], [0:16384]} | slice | bytes 12189696 | tf_op jit(solution)/shard_map/slice | solution.py:29
  22.2 0.3 fusion.3
  22.5 2.1 %multiply_multiply_fusion.1 = (f32[32,16384]{1,0:T(8,128)S(1)}, f32[32,16384]{1,0:T(8,128)S(1)}) fusion(f32[32,16384]{1,0:T(8,128)S(1)} %fusion.3), kind=kOutput, calls=%fused_computation.16 | convolution fusion | flops 203949056 | bytes 6291456 | tf_op jit(solution)/shard_map/dot_general | solution.py:36
  24.6 0.1 slice_add_fusion
  24.7 1.2 copy-done.3
  25.9 3.7 %convolution_bitcast_fusion = f32[3,32,16384]{2,1,0:T(8,128)S(1)} fusion(f32[32,16384]{1,0:T(8,128)S(1)} %get-tuple-element.7, f32[3,32,16384]{2,1,0:T(8,128)S(1)} %bitcast.19, f32[3,1,16384]{2,1,0:T(1,128)S(1)} %collective-permute-done.1, f32[3,31,16384]{2,1,0:T(8,128)S(1)} %slice.40), kind=kOutput, calls=%fused_computation | convolution fusion | flops 608699392 | bytes 20971520 | tf_op jit(solution)/shard_map/ij,cjr->cir/dot_general | solution.py:40
  29.7 2.7 %copy-done.1 = f32[3,32,16384]{2,1,0:T(8,128)} copy-done((f32[3,32,16384]{2,1,0:T(8,128)}, f32[3,32,16384]{2,1,0:T(8,128)S(1)}, u32[]{:S(2)}) %copy-start.1) | copy-done | bytes 6291480
  32.4 0.2 slice.50
  32.6 0.1 copy.14
  32.7 0.8 maximum_bitcast_fusion
  33.6 59.6 %all-gather.4.cloned.1.call-done = f32[32,4,16384]{2,1,0:T(4,128)} async-done(((f32[1,4,16384]{2,1,0:T(4,128)}), f32[32,4,16384]{2,1,0:T(4,128)}) %all-gather.4.cloned.1.call-update) | async-done | bytes 8388624 | tf_op jit(solution)/shard_map/all_gather | solution.py:43
  93.2 4.9 %slice.51 = f32[32,1,16384]{2,1,0:T(1,128)S(1)} slice(f32[32,4,16384]{2,1,0:T(4,128)} %all-gather.4.cloned.1.call-done), slice={[0:32], [0:1], [0:16384]} | slice | bytes 4194304 | tf_op jit(solution)/shard_map/slice | solution.py:44
  98.1 2.5 %copy.13 = f32[32,1,16384]{2,0,1:T(8,128)} copy(f32[32,1,16384]{2,1,0:T(1,128)S(1)} %slice.51) | data formatting | bytes 4194304
  100.6 1.5 select_reduce_fusion.1
  102.1 0.1 copy-done.4
  102.2 2.0 %multiply_multiply_fusion = f32[32,16384]{1,0:T(8,128)} fusion(f32[32,16384]{1,0:T(8,128)S(1)} %fusion.3, f32[32,16384]{1,0:T(8,128)S(1)} %copy-done.4, f32[16384]{0:T(1024)S(1)} %negate_exponential_fusion.2), kind=kLoop, calls=%fused_computation.13 | loop fusion | flops 2621440 | bytes 6356992 | tf_op jit(solution)/shard_map/mul | solution.py:60
  104.2 4.8 %reduce_window_sum.11 = f32[32,16384]{1,0:T(8,128)} reduce-window(f32[32,16384]{1,0:T(8,128)} %bitcast.25, f32[]{:T(128)} %constant.7.clone.1), window={size=32x1 pad=31_0x0_0}, to_apply=%region_0.0 | reduce-window | flops 16252928 | bytes 4194308 | tf_op jit(solution)/shard_map/jit(cumsum)/reduce_window_sum | solution.py:45
  109.0 2.0 %negate_exponential_fusion = f32[32,16384]{1,0:T(8,128)S(1)} fusion(f32[31,16384]{1,0:T(8,128)} %bitcast.26), kind=kLoop, calls=%fused_computation.15 | loop fusion | flops 524288 | bytes 4128768 | tf_op jit(solution)/shard_map/exp | solution.py:47
  111.1 7.8 %select_reduce_fusion = (f32[3,16384]{1,0:T(4,128)S(1)}, f32[3,16384]{1,0:T(4,128)S(1)}) fusion(f32[32,4,16384]{2,1,0:T(4,128)} %all-gather.4.cloned.1.call-done, f32[32,16384]{1,0:T(8,128)S(1)} %negate_exponential_fusion, pred[32]{0:T(512)(128)(4,1)S(1)} %iota_compare_fusion.3), kind=kLoop, calls=%fused_computation.2 | loop fusion | flops 6193152 | bytes 8781856 | tf_op jit(solution)/shard_map/reduce_sum | solution.py:51
  118.9 0.8 multiply_reduce_fusion.1
  119.7 4.5 %multiply_reduce_fusion = f32[32,16384]{1,0:T(8,128)S(1)} fusion(f32[3,32,16384]{2,1,0:T(8,128)} %copy-done.1, f32[16384]{0:T(1024)S(1)} %negate_exponential_fusion.2, f32[3,16384]{1,0:T(4,128)S(1)} %get-tuple-element.6, f32[32,16384]{1,0:T(8,128)S(1)} %copy-done.6, f32[3,16384]{1,0:T(4,128)S(1)} %get-tuple-element.5, f32[3,32,16384]{2,1,0:T(8,128)S(1)} %bitcast.21, ...), kind=kLoop, calls=%fused_computation.5 | loop fusion | flops 12058624 | bytes 23527424 | tf_op jit(solution)/shard_map/reduce_sum | solution.py:61
  124.3 1.3 copy-done.2
  125.7 3.1 %collective-permute-start.2 = (f32[1,16384]{1,0:T(1,128)S(1)}, f32[1,16384]{1,0:T(1,128)S(1)}, u32[]{:S(2)}, u32[]{:S(2)}) collective-permute-start(f32[1,16384]{1,0:T(1,128)S(1)} %slice.54), channel_id=1, source_target_pairs={{0,8},{8,16},{16,24},{24,32},{32,40},{40,48},{48,56},{56,64},{64,7... | collective-permute-start | bytes 196616 | tf_op jit(solution)/shard_map/ppermute | solution.py:10
  128.7 0.7 broadcast_in_dim.50
  129.4 13.1 %all_to_all.6 = f32[8,1,1]{2,1,0:T(1,128)S(1)} all-to-all(f32[8,1,1]{2,1,0:T(1,128)S(1)} %broadcast_in_dim.50), channel_id=1, replica_groups=mesh['depth'=32,'rays'=8] {'rays'}, dimensions={0} | all-to-all | bytes 64 | tf_op jit(solution)/shard_map/all_to_all | solution.py:15
  142.5 0.6 reduce_sum.59
  143.7 3.9 %fusion.4 = f32[32,16384]{1,0:T(8,128)} fusion(f32[32,16384]{1,0:T(8,128)} %copy-done.2, f32[31,16384]{1,0:T(8,128)} %bitcast.24, f32[1,16384]{1,0:T(1,128)S(1)} %collective-permute-done.2), kind=kLoop, calls=%fused_computation.11 | loop fusion | flops 1572864 | bytes 6291456 | tf_op jit(solution)/shard_map/mul | solution.py:63
  (35 shorter events, 0.2 us)
Async XLA Ops:
  7.2 86.0 %all-gather.4.cloned.1.call-start = ((), (), s32[]{:S(2)}) async-start(), calls=%async_computation.1 | async-start | bytes 8650752 | tf_op jit(solution)/shard_map/all_gather | solution.py:43
  8.3 13.9 %collective-permute-start = (f32[1,16384]{1,0:T(1,128)S(1)}, f32[1,16384]{1,0:T(1,128)S(1)}, u32[]{:S(2)}, u32[]{:S(2)}) collective-permute-start(f32[1,16384]{1,0:T(1,128)S(1)} %slice.37), channel_id=1, source_target_pairs={{8,0},{16,8},{24,16},{32,24},{40,32},{48,40},{56,48},{64,56},{72,6... | collective-permute-start | bytes 196616 | tf_op jit(solution)/shard_map/ppermute | solution.py:10
  14.9 9.8 %collective-permute-start.1 = (f32[3,1,16384]{2,1,0:T(1,128)S(1)}, f32[3,1,16384]{2,1,0:T(1,128)S(1)}, u32[]{:S(2)}, u32[]{:S(2)}) collective-permute-start(f32[3,1,16384]{2,1,0:T(1,128)S(1)} %slice.41), channel_id=1, source_target_pairs={{8,0},{16,8},{24,16},{32,24},{40,32},{48,40},{56,48},{64,56},{72,6... | collective-permute-start | bytes 589832 | tf_op jit(solution)/shard_map/ppermute | solution.py:10
  18.6 3.6 %copy-start.5 = (f32[32,16384]{1,0:T(8,128)S(1)}, f32[32,16384]{1,0:T(8,128)}, u32[]{:S(2)}) copy-start(f32[32,16384]{1,0:T(8,128)} %param.3) | copy-start | bytes 6291460
  18.6 7.3 %slice-start = ((s8[6291456]{0:T(1024)(128)(4,1)}), s8[4194304]{0:T(1024)(128)(4,1)S(1)}, s32[]{:S(2)}) async-start(s8[6291456]{0:T(1024)(128)(4,1)} %bitcast.18), calls=%async_computation.2 | async-start | bytes 8388608
  22.2 3.7 %copy-start = (f32[3,31,16384]{2,1,0:T(8,128)}, f32[3,31,16384]{2,1,0:T(8,128)S(1)}, u32[]{:S(2)}) copy-start(f32[3,31,16384]{2,1,0:T(8,128)S(1)} %slice.40) | copy-start | bytes 18284548
  22.2 3.7 %slice-start.1 = ((s8[6291456]{0:T(1024)(128)(4,1)}), s8[2097152]{0:T(1024)(128)(4,1)S(1)}, s32[]{:S(2)}) async-start(s8[6291456]{0:T(1024)(128)(4,1)} %bitcast.18), calls=%async_computation.3 | async-start | bytes 4194304
  24.6 1.3 copy-start.3
  29.7 2.7 %copy-start.1 = (f32[3,32,16384]{2,1,0:T(8,128)}, f32[3,32,16384]{2,1,0:T(8,128)S(1)}, u32[]{:S(2)}) copy-start(f32[3,32,16384]{2,1,0:T(8,128)S(1)} %convolution_bitcast_fusion) | copy-start | bytes 18874372
  100.6 1.6 %copy-start.4 = (f32[32,16384]{1,0:T(8,128)S(1)}, f32[32,16384]{1,0:T(8,128)}, u32[]{:S(2)}) copy-start(f32[32,16384]{1,0:T(8,128)} %copy-done.3) | copy-start | bytes 6291460
  104.2 15.4 %slice-start.4 = ((s8[6291456]{0:T(1024)(128)(4,1)}), s8[2097152]{0:T(1024)(128)(4,1)S(1)}, s32[]{:S(2)}) async-start(s8[6291456]{0:T(1024)(128)(4,1)} %bitcast.22), calls=%async_computation.6 | async-start | bytes 4194304
  109.0 10.6 %slice-start.2 = ((s8[6291456]{0:T(1024)(128)(4,1)}), s8[4194304]{0:T(1024)(128)(4,1)S(1)}, s32[]{:S(2)}) async-start(s8[6291456]{0:T(1024)(128)(4,1)} %bitcast.20), calls=%async_computation.4 | async-start | bytes 8388608
  111.1 7.8 %copy-start.7 = (f32[3,16384]{1,0:T(4,128)S(1)}, f32[3,16384]{1,0:T(4,128)}, u32[]{:S(2)}) copy-start(f32[3,16384]{1,0:T(4,128)} %param.5) | copy-start | bytes 589828
  111.1 8.6 %slice-start.3 = ((s8[6291456]{0:T(1024)(128)(4,1)}), s8[2097152]{0:T(1024)(128)(4,1)S(1)}, s32[]{:S(2)}) async-start(s8[6291456]{0:T(1024)(128)(4,1)} %bitcast.20), calls=%async_computation.5 | async-start | bytes 4194304
  111.1 8.6 %slice-start.5 = ((s8[6291456]{0:T(1024)(128)(4,1)}), s8[4194304]{0:T(1024)(128)(4,1)S(1)}, s32[]{:S(2)}) async-start(s8[6291456]{0:T(1024)(128)(4,1)} %bitcast.22), calls=%async_computation.7 | async-start | bytes 8388608
  111.1 8.6 %copy-start.6 = (f32[32,16384]{1,0:T(8,128)S(1)}, f32[32,16384]{1,0:T(8,128)}, u32[]{:S(2)}) copy-start(f32[32,16384]{1,0:T(8,128)} %multiply_multiply_fusion) | copy-start | bytes 6291460
  124.3 1.3 copy-start.2
  125.7 18.1 %collective-permute-start.2 = (f32[1,16384]{1,0:T(1,128)S(1)}, f32[1,16384]{1,0:T(1,128)S(1)}, u32[]{:S(2)}, u32[]{:S(2)}) collective-permute-start(f32[1,16384]{1,0:T(1,128)S(1)} %slice.54), channel_id=1, source_target_pairs={{0,8},{8,16},{16,24},{24,32},{32,40},{40,48},{48,56},{56,64},{64,7... | collective-permute-start | bytes 196616 | tf_op jit(solution)/shard_map/ppermute | solution.py:10
Sparse Core Ops, SparseCore 0:
  33.7 59.4 all-gather.3
where the time goes:
time: 156 us
  waiting for transfers between devices  59.6 us (38%)
  other arithmetic  29.1 us (19%)
  local copies, waits for them, and re-layouts  21.7 us (14%)
  between operations  16.1 us (10%)
  blocking collectives  13.1 us (8%)
  starting transfers between devices  10.1 us (6%)
  matrix products  5.85 us (4%)
    all_gather x1, waiting for transfers between devices, on_device(): all_slabs = lax.all_gather(stacked, 'depth', axis=0, tiled=True)  59.6 us
    all_to_all x1, blocking collectives, copy_for_each(): lax.all_to_all(jnp.broadcast_to(shard[None], (size, *shard.shape)), axis,...  13.1 us
    ppermute x3, starting transfers between devices, shifted(): lax.ppermute(value, axis, [(source, source + steps) for source in range(i...  10.1 us
    unnamed x30, local copies, waits for them, and re-layouts  8.03 us
    reduce_sum x1, other arithmetic, on_device(): jnp.sum(jnp.where(earlier_mask[:, None, None], weighted, 0.0), axis=0)  7.77 us
    slice x1, local copies, waits for them, and re-layouts, on_device(): depths = all_slabs[:, 0]  4.9 us
    another operation x1, other arithmetic, on_device(): depth_running = jnp.cumsum(depths, axis=0)  4.81 us
    reduce_sum x1, other arithmetic, on_device(): sample_grad = jnp.sum(residual_grad[:, None, :] * bracket, axis=0)  4.54 us
  transfers between devices with their start and end apart: 4, of which 1 were waited for; matrix products, arithmetic and copies ran while one was open for 7% of the time, Pallas kernels for 0%

commit v1 on v0

v1 whole, which is shorter than its diff:
```python
import jax
import jax.numpy as jnp
from jax import lax
from jax.experimental import pallas as pl
from jax.experimental.pallas import tpu as pltpu
from jax.sharding import PartitionSpec as P

SLABS = 32
SAMPLES = 32
EIGHTS = SAMPLES // 8
TILES = 128
LANES = 128
OWNED = TILES // SLABS
GROUP = 8
SENT = 12
LOSS = 6 * OWNED
ANSWER = 8 * OWNED
F32 = jnp.float32
MIB = 1 << 20
LARGE = 59
WHOLE = pl.BlockSpec(memory_space=pltpu.VMEM)
FAR = pl.BlockSpec(memory_space=pltpu.HBM)


def call(kernel, name, in_specs, out_specs, out_shape, scratch, mib, flops=0):
    return pl.pallas_call(
        kernel,
        in_specs=in_specs,
        out_specs=out_specs,
        out_shape=out_shape,
        scratch_shapes=scratch,
        compiler_params=pltpu.CompilerParams(vmem_limit_bytes=mib * MIB),
        cost_estimate=pl.CostEstimate(flops=flops, bytes_accessed=8 * MIB, transcendentals=0),
        name=name,
    )


def tiled_view(block):
    lead = block.shape[:-2]
    cut = block.reshape(*lead, EIGHTS, 8, TILES, LANES)
    return jnp.swapaxes(cut, -3, -2).reshape(-1, TILES * 8, LANES)


def untiled_view(block):
    cut = block.reshape(EIGHTS, TILES, 8, LANES)
    return jnp.swapaxes(cut, 1, 2).reshape(SAMPLES, TILES * LANES)


def sample_place(sample, base):
    return pl.ds(pl.multiple_of(base * 8, 64) + sample % 8, GROUP, stride=8)


def sample_row(ref, channel, sample, base):
    return ref[channel * EIGHTS + sample // 8, sample_place(sample, base), :]


def fetches(pairs, sems):
    chunks = sems.shape[0]
    size = TILES * 8 // chunks
    return [
        [
            pltpu.make_async_copy(a.at[:, pl.ds(k * size, size)], b.at[:, pl.ds(k * size, size)], sems.at[k, n])
            for n, (a, b) in enumerate(pairs)
        ]
        for k in range(chunks)
    ]


def start_all(copies):
    for some in copies:
        for copy in some:
            copy.start()


def wait_all(copies):
    for some in copies:
        for copy in some:
            copy.wait()


def in_chunks(arrivals, departures, count, one):
    start_all(arrivals)
    each = count // len(arrivals)
    for k, some in enumerate(arrivals):
        wait_all([some])
        lax.fori_loop(k * each, (k + 1) * each, one, 0)
        start_all([departures[k]])
    wait_all(departures)


def inner_kernel(density_in, radiance_in, out, density, radiance, sent, sems, out_sems):
    chunks = sems.shape[0]
    owners = SLABS // chunks

    def one_group(group, carry):
        base = pl.multiple_of(group * GROUP, GROUP)
        first = here = sample_row(density, 0, 0, base)
        color = [sample_row(radiance, c, 0, base) for c in range(3)]
        before = first_color = color
        doubled = jnp.zeros((GROUP, LANES), F32)
        total = None
        half = None
        for i in range(SAMPLES - 1):
            nxt = sample_row(density, 0, i + 1, base)
            after = [sample_row(radiance, c, i + 1, base) for c in range(3)]
            if i == 0:
                total = [0.5 * (color[c] + after[c]) for c in range(3)]
            else:
                total = [total[c] + half * (after[c] - before[c]) for c in range(3)]
            doubled = doubled + (here + nxt)
            half = 0.5 * jnp.exp(-0.5 * doubled)
            before, color, here = color, after, nxt
        known = [total[c] - half * before[c] for c in range(3)]
        parts = [doubled, here, first] + known + color + first_color
        for q in range(SENT):
            for k in range(GROUP // OWNED):
                owner = group * (GROUP // OWNED) + k
                sent[owner, q * OWNED : (q + 1) * OWNED, :] = parts[q][k * OWNED : (k + 1) * OWNED, :]
        return carry

    arrivals = fetches([(density_in, density), (radiance_in, radiance)], sems)
    departures = [
        [
            pltpu.make_async_copy(
                sent.at[pl.ds(k * owners, owners)], out.at[pl.ds(k * owners, owners)], out_sems.at[k]
            )
        ]
        for k in range(chunks)
    ]
    in_chunks(arrivals, departures, TILES // GROUP, one_group)


def inner(density, radiance, chunks=8):
    shape = (SLABS, SENT * OWNED, LANES)
    return call(
        inner_kernel,
        "slab_inner",
        [FAR, FAR],
        FAR,
        jax.ShapeDtypeStruct(shape, F32),
        [
            pltpu.VMEM((EIGHTS, TILES * 8, LANES), F32),
            pltpu.VMEM((3 * EIGHTS, TILES * 8, LANES), F32),
            pltpu.VMEM(shape, F32),
            pltpu.SemaphoreType.DMA((chunks, 2)),
            pltpu.SemaphoreType.DMA((chunks,)),
        ],
        LARGE,
    )(density, radiance)


def scan_kernel(owner, slabs, target, out):
    def value(s, q):
        return slabs[s, q * OWNED : (q + 1) * OWNED, :]

    zero = jnp.zeros((OWNED, LANES), F32)
    start = zero
    pixel = [zero] * 3
    offsets, befores, ends = [], [], []
    for s in range(SLABS):
        more = s < SLABS - 1
        doubled = value(s, 0)
        depth = 0.5 * (doubled + value(s, 1) + (value(s + 1, 2) if more else zero))
        half = 0.5 * jnp.exp(-0.5 * doubled)
        behind = 0.5 * jnp.exp(-depth)
        offset = jnp.exp(-start)
        end = []
        befores.append(pixel)
        following = []
        for c in range(3):
            after = value(s + 1, 9 + c) if more else zero
            last = value(s, 3 + c) + half * after
            end.append(offset * last)
            following.append(pixel[c] + offset * (last - behind * (value(s, 6 + c) + after)))
        pixel = following
        offsets.append(offset)
        ends.append(end)
        start = start + depth
    first = owner[0] * (OWNED * LANES)
    error = []
    for c in range(3):
        rows = [
            target[c : c + 1, pl.ds(pl.multiple_of(first + k * LANES, LANES), LANES)]
            for k in range(OWNED)
        ]
        error.append(pixel[c] - jnp.concatenate(rows, axis=0))
    residual = [2.0 * e for e in error]
    loss = error[0] * error[0] + error[1] * error[1] + error[2] * error[2]
    previous = zero
    for s in range(SLABS):
        left = [residual[c] * (pixel[c] - befores[s][c]) for c in range(3)]
        left = left[0] + left[1] + left[2]
        last = [residual[c] * ends[s][c] for c in range(3)]
        last = last[0] + last[1] + last[2] - left
        answer = [offsets[s] * residual[c] for c in range(3)]
        answer += [left, 0.5 * (left - previous), 0.5 * (left - last), loss, zero]
        for q, part in enumerate(answer):
            out[s, q * OWNED : (q + 1) * OWNED, :] = part
        previous = last


def scan_slabs(owner, slabs, target):
    return call(
        scan_kernel,
        "scan_slabs",
        [pl.BlockSpec(memory_space=pltpu.SMEM), WHOLE, WHOLE],
        WHOLE,
        jax.ShapeDtypeStruct((SLABS, ANSWER, LANES), F32),
        [],
        6,
    )(owner, slabs, target)


def halves_kernel(density_in, radiance_in, out, density, radiance, halves, sems, out_sems):
    def one_group(group, carry):
        base = pl.multiple_of(group * GROUP, GROUP)
        here = sample_row(density, 0, 0, base)
        color = [sample_row(radiance, c, 0, base) for c in range(3)]
        before = color
        doubled = jnp.zeros((GROUP, LANES), F32)
        half = None
        for i in range(SAMPLES):
            store = half
            if i < SAMPLES - 1:
                after = [sample_row(radiance, c, i + 1, base) for c in range(3)]
                if i == 0:
                    half = [0.25 * (color[c] + after[c]) for c in range(3)]
                    store = half
                else:
                    transmit = 0.25 * jnp.exp(-0.5 * doubled)
                    new = [half[c] + transmit * (after[c] - before[c]) for c in range(3)]
                    store = [half[c] + new[c] for c in range(3)]
                    half = new
                nxt = sample_row(density, 0, i + 1, base)
                doubled = doubled + (here + nxt)
                here, before, color = nxt, color, after
            for c in range(3):
                halves[c * EIGHTS + i // 8, sample_place(i, base), :] = store[c]
        return carry

    arrivals = fetches([(density_in, density), (radiance_in, radiance)], sems)
    in_chunks(arrivals, fetches([(halves, out)], out_sems), TILES // GROUP, one_group)


def halves_of(density, radiance, chunks=8):
    shape = (3 * EIGHTS, TILES * 8, LANES)
    return call(
        halves_kernel,
        "slab_halves",
        [FAR, FAR],
        FAR,
        jax.ShapeDtypeStruct(shape, F32),
        [
            pltpu.VMEM((EIGHTS, TILES * 8, LANES), F32),
            pltpu.VMEM(shape, F32),
            pltpu.VMEM(shape, F32),
            pltpu.SemaphoreType.DMA((chunks, 2)),
            pltpu.SemaphoreType.DMA((chunks, 1)),
        ],
        LARGE,
        1_000_000_000,
    )(density, radiance)


def loss_kernel(back, out):
    total = back[0, LOSS : LOSS + OWNED, :]
    for s in range(1, SLABS):
        total = total + back[s, LOSS : LOSS + OWNED, :]
    total = jnp.sum(total, axis=0, keepdims=True)
    for z in range(out.shape[0]):
        out[z] = total


def tile_loss(back, count):
    return call(
        loss_kernel,
        "tile_loss",
        [WHOLE],
        WHOLE,
        jax.ShapeDtypeStruct((count, 1, LANES), F32),
        [],
        4,
    )(back)


def gradient_kernel(halves_in, back, out, halves, held, sems, out_sems):
    sample = lax.broadcasted_iota(jnp.int32, (8, LANES), 0)

    def one_owner(owner, carry):
        for k in range(OWNED):
            rows = pl.ds(pl.multiple_of(owner * (OWNED * 8), OWNED * 8) + k * 8, 8)
            known = [
                jnp.broadcast_to(back[owner, q * OWNED + k : q * OWNED + k + 1, :], (8, LANES))
                for q in range(6)
            ]
            for a in range(EIGHTS):
                value = known[0] * halves[a, rows, :]
                value += known[1] * halves[EIGHTS + a, rows, :]
                value += known[2] * halves[2 * EIGHTS + a, rows, :]
                left = known[3]
                if a == 0:
                    left = jnp.where(sample == 0, known[4], left)
                if a == EIGHTS - 1:
                    left = jnp.where(sample == 7, known[5], left)
                held[a, rows, :] = value - left
        return carry

    arrivals = fetches([(halves_in, halves)], sems)
    in_chunks(arrivals, fetches([(held, out)], out_sems), SLABS, one_owner)


def gradient(halves, back, chunks=8):
    shape = (EIGHTS, TILES * 8, LANES)
    return call(
        gradient_kernel,
        "slab_gradient",
        [FAR, WHOLE],
        FAR,
        jax.ShapeDtypeStruct(shape, F32),
        [
            pltpu.VMEM((3 * EIGHTS, TILES * 8, LANES), F32),
            pltpu.VMEM(shape, F32),
            pltpu.SemaphoreType.DMA((chunks, 1)),
            pltpu.SemaphoreType.DMA((chunks, 1)),
        ],
        LARGE,
        1_000_000_000,
    )(halves, back)


def on_device(density, radiance, target):
    density, radiance = tiled_view(density), tiled_view(radiance)
    owner = lax.axis_index("depth").astype(jnp.int32)[None]
    slabs = lax.all_to_all(inner(density, radiance), "depth", 0, 0, tiled=True)
    answers = scan_slabs(owner, slabs, target)
    back = lax.all_to_all(answers, "depth", 0, 0, tiled=True)
    halves = halves_of(density, radiance)
    zs = lax.axis_size("rays")
    losses = lax.all_to_all(tile_loss(back, zs), "rays", 0, 0, tiled=True)
    grad = gradient(halves, back)
    loss_mean = jnp.sum(losses) / (3.0 * zs * TILES * LANES)
    return untiled_view(grad), loss_mean


def solution(mesh):
    in_specs = (P("depth", "rays"), P(None, "depth", "rays"), P(None, "rays"))
    out_specs = (P("depth", "rays"), P())
    return jax.shard_map(
        on_device, mesh=mesh, in_specs=in_specs, out_specs=out_specs, check_vma=False
    )
```

time: 156 us -> 62.9 us (0.40)
  waiting for transfers between devices: 59.6 us -> 21 us
  other arithmetic: 29.1 us -> 0.61 us
  local copies, waits for them, and re-layouts: 21.7 us -> 0.01 us
  Pallas kernels: 0 us -> 17.9 us
  between operations: 16.1 us -> 2.47 us
  blocking collectives: 13.1 us -> 0 us
  starting transfers between devices: 10.1 us -> 20.6 us
  matrix products: 5.85 us -> 0 us
    all_gather x1 -> x0, waiting for transfers between devices: 59.6 us -> none  [on_device(): all_slabs = lax.all_gather(stacked, 'depth', axis=0, tiled=True)]
    all_to_all x0 -> x3, waiting for transfers between devices: none -> 21 us  [the longest x1 14.2 us: on_device(): slabs = lax.all_to_all(inner(density, radiance), 'depth', 0, 0, tiled=True)]
    all_to_all x0 -> x3, starting transfers between devices: none -> 20.6 us  [the longest x1 8.59 us: on_device(): slabs = lax.all_to_all(inner(density, radiance), 'depth', 0, 0, tiled=True)]
    pallas_call x0 -> x5, Pallas kernels: none -> 17.9 us  [the longest x1 6.19 us: halves_of(): call(halves_kernel, 'slab_halves', [FAR, FAR], FAR, jax.ShapeDtypeStruct(...]
    reduce_sum x5 -> x1, other arithmetic: 15.1 us -> 0.61 us  [on_device(): loss_mean = jnp.sum(losses) / (3.0 * zs * TILES * LANES)]
    all_to_all x1 -> x0, blocking collectives: 13.1 us -> none  [copy_for_each(): lax.all_to_all(jnp.broadcast_to(shard[None], (size, *shard.shape)), axis,...]
    slice x7 -> x0, local copies, waits for them, and re-layouts: 13 us -> none  [the longest x1 4.9 us: on_device(): depths = all_slabs[:, 0]]
    ppermute x3 -> x0, starting transfers between devices: 10.1 us -> none  [shifted(): lax.ppermute(value, axis, [(source, source + steps) for source in range(i...]
  transfers between devices with their start and end apart: 4 -> 3, of which waited for: 1 -> 3; matrix products, arithmetic and copies ran while one was open for 7% -> 0% of each run, Pallas kernels for 0% -> 18%
where the time goes in v1:
time: 62.9 us; the launch traced here: 62.5 us
  waiting for transfers between devices  21 us (33%)
  starting transfers between devices  20.6 us (33%)
  Pallas kernels  17.9 us (28%)
  between operations  2.47 us (4%)
    all_to_all x1, waiting for transfers between devices, on_device(): slabs = lax.all_to_all(inner(density, radiance), 'depth', 0, 0, tiled=True)  14.2 us
    all_to_all x1, starting transfers between devices, on_device(): slabs = lax.all_to_all(inner(density, radiance), 'depth', 0, 0, tiled=True)  8.59 us
    all_to_all x1, starting transfers between devices, on_device(): losses = lax.all_to_all(tile_loss(back, zs), 'rays', 0, 0, tiled=True)  8.19 us
    pallas_call x1, Pallas kernels, halves_of(): call(halves_kernel, 'slab_halves', [FAR, FAR], FAR, jax.ShapeDtypeStruct(...  6.19 us
    all_to_all x1, waiting for transfers between devices, on_device(): back = lax.all_to_all(answers, 'depth', 0, 0, tiled=True)  5.4 us
    pallas_call x1, Pallas kernels, gradient(): call(gradient_kernel, 'slab_gradient', [FAR, WHOLE], FAR, jax.ShapeDtypeS...  5.23 us
    pallas_call x1, Pallas kernels, inner(): call(inner_kernel, 'slab_inner', [FAR, FAR], FAR, jax.ShapeDtypeStruct(sh...  4.64 us
    all_to_all x1, starting transfers between devices, on_device(): back = lax.all_to_all(answers, 'depth', 0, 0, tiled=True)  3.79 us
  transfers between devices with their start and end apart: 3, of which 3 were waited for; matrix products, arithmetic and copies ran while one was open for 0% of the time, Pallas kernels for 18%

profile of v1, /device:TPU:1, one launch (start us, length us, event | category | flops | bytes accessed | tf_op | source)
XLA Modules:
  0.0 62.5 jit_solution(16593038304862592357)
XLA Ops:
  0.6 0.0 copy-start.1
  0.6 4.6 %slab_inner.1 = f32[32,48,128]{2,1,0:T(8,128)} custom-call(f32[4,1024,128]{2,1,0:T(8,128)} %bitcast.18, f32[12,1024,128]{2,1,0:T(8,128)} %bitcast.16), custom_call_target="tpu_custom_call" | custom-call | bytes 8388608 | tf_op jit(solution)/shard_map/slab_inner/pallas_call | solution.py:135
  5.3 8.6 %all-to-all-start = ((f32[32,48,128]{2,1,0:T(8,128)}), f32[32,48,128]{2,1,0:T(8,128)S(1)}, u32[]{:S(2)}, u32[]{:S(2)}) async-start(f32[32,48,128]{2,1,0:T(8,128)} %slab_inner.1), calls=%async_computation | async-start | bytes 1572864 | tf_op jit(solution)/shard_map/all_to_all | solution.py:334
  13.9 14.2 %all-to-all-done.slabs = f32[32,48,128]{2,1,0:T(8,128)S(1)} async-done(((f32[32,48,128]{2,1,0:T(8,128)}), f32[32,48,128]{2,1,0:T(8,128)S(1)}, u32[]{:S(2)}, u32[]{:S(2)}) %all-to-all-start) | async-done | bytes 786464 | tf_op jit(solution)/shard_map/all_to_all | solution.py:334
  28.1 0.0 copy-done.1
  28.1 1.1 %scan_slabs.1 = f32[32,32,128]{2,1,0:T(8,128)} custom-call(s32[1]{0:T(128)} %bitcast.6.owner, f32[32,48,128]{2,1,0:T(8,128)S(1)} %all-to-all-done.slabs, f32[3,16384]{1,0:T(4,128)S(1)} %copy-done.1), custom_call_target="tpu_custom_call" | custom-call | bytes 8388608 | tf_op jit(solution)/shard_map/scan_slabs/pallas_call | solution.py:203
  29.3 3.8 %all-to-all-start.1 = ((f32[32,32,128]{2,1,0:T(8,128)}), f32[32,32,128]{2,1,0:T(8,128)S(1)}, u32[]{:S(2)}, u32[]{:S(2)}) async-start(f32[32,32,128]{2,1,0:T(8,128)} %scan_slabs.1), calls=%async_computation.1 | async-start | bytes 1048576 | tf_op jit(solution)/shard_map/all_to_all | solution.py:336
  33.1 6.2 %slab_halves.1.halves_in = f32[12,1024,128]{2,1,0:T(8,128)} custom-call(f32[4,1024,128]{2,1,0:T(8,128)} %bitcast.19, f32[12,1024,128]{2,1,0:T(8,128)} %bitcast.17), custom_call_target="tpu_custom_call" | custom-call | flops 1000000000 | bytes 8388608 | tf_op jit(solution)/shard_map/slab_halves/pallas_call | solution.py:247
  39.2 5.4 %all-to-all-done.1.back = f32[32,32,128]{2,1,0:T(8,128)S(1)} async-done(((f32[32,32,128]{2,1,0:T(8,128)}), f32[32,32,128]{2,1,0:T(8,128)S(1)}, u32[]{:S(2)}, u32[]{:S(2)}) %all-to-all-start.1) | async-done | bytes 524320 | tf_op jit(solution)/shard_map/all_to_all | solution.py:336
  44.6 0.0 copy-start
  44.6 0.7 %tile_loss.1 = f32[8,1,128]{2,1,0:T(1,128)} custom-call(f32[32,32,128]{2,1,0:T(8,128)S(1)} %all-to-all-done.1.back), custom_call_target="tpu_custom_call" | custom-call | bytes 8388608 | tf_op jit(solution)/shard_map/tile_loss/pallas_call | solution.py:275
  45.4 8.2 %all-to-all-start.2 = ((f32[8,1,128]{2,1,0:T(1,128)}), f32[8,1,128]{2,1,0:T(1,128)S(1)}, u32[]{:S(2)}, u32[]{:S(2)}) async-start(f32[8,1,128]{2,1,0:T(1,128)} %tile_loss.1), calls=%async_computation.2 | async-start | bytes 8192 | tf_op jit(solution)/shard_map/all_to_all | solution.py:339
  53.6 0.0 copy-done
  53.6 5.2 %slab_gradient.1 = f32[4,1024,128]{2,1,0:T(8,128)} custom-call(f32[12,1024,128]{2,1,0:T(8,128)} %slab_halves.1.halves_in, f32[32,32,128]{2,1,0:T(8,128)} %copy-done), custom_call_target="tpu_custom_call" | custom-call | flops 1000000000 | bytes 8388608 | tf_op jit(solution)/shard_map/slab_gradient/pallas_call | solution.py:314
  58.8 1.3 %all-to-all-done.2 = f32[8,1,128]{2,1,0:T(1,128)S(1)} async-done(((f32[8,1,128]{2,1,0:T(1,128)}), f32[8,1,128]{2,1,0:T(1,128)S(1)}, u32[]{:S(2)}, u32[]{:S(2)}) %all-to-all-start.2) | async-done | bytes 4128 | tf_op jit(solution)/shard_map/all_to_all | solution.py:339
  60.1 0.6 reduce_sum.9
Async XLA Ops:
  0.6 27.5 %copy-start.1 = (f32[3,16384]{1,0:T(4,128)S(1)}, f32[3,16384]{1,0:T(4,128)}, u32[]{:S(2)}) copy-start(f32[3,16384]{1,0:T(4,128)} %target.1) | copy-start | bytes 589828
  5.3 22.8 %all-to-all-start = ((f32[32,48,128]{2,1,0:T(8,128)}), f32[32,48,128]{2,1,0:T(8,128)S(1)}, u32[]{:S(2)}, u32[]{:S(2)}) async-start(f32[32,48,128]{2,1,0:T(8,128)} %slab_inner.1), calls=%async_computation | async-start | bytes 1572864 | tf_op jit(solution)/shard_map/all_to_all | solution.py:334
  29.3 15.4 %all-to-all-start.1 = ((f32[32,32,128]{2,1,0:T(8,128)}), f32[32,32,128]{2,1,0:T(8,128)S(1)}, u32[]{:S(2)}, u32[]{:S(2)}) async-start(f32[32,32,128]{2,1,0:T(8,128)} %scan_slabs.1), calls=%async_computation.1 | async-start | bytes 1048576 | tf_op jit(solution)/shard_map/all_to_all | solution.py:336
  44.6 8.9 %copy-start = (f32[32,32,128]{2,1,0:T(8,128)}, f32[32,32,128]{2,1,0:T(8,128)S(1)}, u32[]{:S(2)}) copy-start(f32[32,32,128]{2,1,0:T(8,128)S(1)} %all-to-all-done.1.back) | copy-start | bytes 1572868
  45.4 14.8 %all-to-all-start.2 = ((f32[8,1,128]{2,1,0:T(1,128)}), f32[8,1,128]{2,1,0:T(1,128)S(1)}, u32[]{:S(2)}, u32[]{:S(2)}) async-start(f32[8,1,128]{2,1,0:T(1,128)} %tile_loss.1), calls=%async_computation.2 | async-start | bytes 8192 | tf_op jit(solution)/shard_map/all_to_all | solution.py:339

commit v2 on v1

--- a/solution.py
+++ b/solution.py
@@ -1,3 +1,5 @@
+import functools
+
 import jax
 import jax.numpy as jnp
 from jax import lax
@@ -14,10 +16,11 @@
 GROUP = 8
 SENT = 12
 LOSS = 6 * OWNED
-ANSWER = 8 * OWNED
+ANSWER = LOSS + 1
 F32 = jnp.float32
 MIB = 1 << 20
-LARGE = 59
+INNER_MIB, HALVES_MIB, GRADIENT_MIB = 52, 49.5, 50
+NEAR = 48
 WHOLE = pl.BlockSpec(memory_space=pltpu.VMEM)
 FAR = pl.BlockSpec(memory_space=pltpu.HBM)
 
@@ -29,8 +32,8 @@
         out_specs=out_specs,
         out_shape=out_shape,
         scratch_shapes=scratch,
-        compiler_params=pltpu.CompilerParams(vmem_limit_bytes=mib * MIB),
-        cost_estimate=pl.CostEstimate(flops=flops, bytes_accessed=8 * MIB, transcendentals=0),
+        compiler_params=pltpu.CompilerParams(vmem_limit_bytes=int(mib * MIB)),
+        cost_estimate=pl.CostEstimate(flops=flops, bytes_accessed=1024, transcendentals=0),
         name=name,
     )
 
@@ -56,7 +59,7 @@
 
 def fetches(pairs, sems):
     chunks = sems.shape[0]
-    size = TILES * 8 // chunks
+    size = pairs[0][0].shape[1] // chunks
     return [
         [
             pltpu.make_async_copy(a.at[:, pl.ds(k * size, size)], b.at[:, pl.ds(k * size, size)], sems.at[k, n])
@@ -84,14 +87,13 @@
     for k, some in enumerate(arrivals):
         wait_all([some])
         lax.fori_loop(k * each, (k + 1) * each, one, 0)
-        start_all([departures[k]])
-    wait_all(departures)
-
-
-def inner_kernel(density_in, radiance_in, out, density, radiance, sent, sems, out_sems):
-    chunks = sems.shape[0]
-    owners = SLABS // chunks
-
+        if departures:
+            start_all([departures[k]])
+    if departures:
+        wait_all(departures)
+
+
+def inner_kernel(owner, density_in, radiance_in, sent, density, radiance, sems):
     def one_group(group, carry):
         base = pl.multiple_of(group * GROUP, GROUP)
         first = here = sample_row(density, 0, 0, base)
@@ -119,34 +121,24 @@
         return carry
 
     arrivals = fetches([(density_in, density), (radiance_in, radiance)], sems)
-    departures = [
-        [
-            pltpu.make_async_copy(
-                sent.at[pl.ds(k * owners, owners)], out.at[pl.ds(k * owners, owners)], out_sems.at[k]
-            )
-        ]
-        for k in range(chunks)
-    ]
-    in_chunks(arrivals, departures, TILES // GROUP, one_group)
-
-
-def inner(density, radiance, chunks=8):
+    in_chunks(arrivals, None, TILES // GROUP, one_group)
+
+
+def inner(owner, density, radiance, chunks=8):
     shape = (SLABS, SENT * OWNED, LANES)
     return call(
         inner_kernel,
         "slab_inner",
-        [FAR, FAR],
-        FAR,
+        [pl.BlockSpec(memory_space=pltpu.SMEM), FAR, FAR],
+        WHOLE,
         jax.ShapeDtypeStruct(shape, F32),
         [
             pltpu.VMEM((EIGHTS, TILES * 8, LANES), F32),
             pltpu.VMEM((3 * EIGHTS, TILES * 8, LANES), F32),
-            pltpu.VMEM(shape, F32),
             pltpu.SemaphoreType.DMA((chunks, 2)),
-            pltpu.SemaphoreType.DMA((chunks,)),
-        ],
-        LARGE,
-    )(density, radiance)
+        ],
+        INNER_MIB,
+    )(owner, density, radiance)
 
 
 def scan_kernel(owner, slabs, target, out):
@@ -186,6 +178,7 @@
         error.append(pixel[c] - jnp.concatenate(rows, axis=0))
     residual = [2.0 * e for e in error]
     loss = error[0] * error[0] + error[1] * error[1] + error[2] * error[2]
+    loss = jnp.sum(loss, axis=0, keepdims=True)
     previous = zero
     for s in range(SLABS):
         left = [residual[c] * (pixel[c] - befores[s][c]) for c in range(3)]
@@ -193,9 +186,11 @@
         last = [residual[c] * ends[s][c] for c in range(3)]
         last = last[0] + last[1] + last[2] - left
         answer = [offsets[s] * residual[c] for c in range(3)]
-        answer += [left, 0.5 * (left - previous), 0.5 * (left - last), loss, zero]
+        answer += [left, 0.5 * (left - previous), 0.5 * (left - last)]
+        top = s * ANSWER
         for q, part in enumerate(answer):
-            out[s, q * OWNED : (q + 1) * OWNED, :] = part
+            out[top + q * OWNED : top + (q + 1) * OWNED, :] = part
+        out[top + LOSS : top + ANSWER, :] = loss
         previous = last
 
 
@@ -205,14 +200,14 @@
         "scan_slabs",
         [pl.BlockSpec(memory_space=pltpu.SMEM), WHOLE, WHOLE],
         WHOLE,
-        jax.ShapeDtypeStruct((SLABS, ANSWER, LANES), F32),
+        jax.ShapeDtypeStruct((SLABS * ANSWER, LANES), F32),
         [],
         6,
     )(owner, slabs, target)
 
 
-def halves_kernel(density_in, radiance_in, out, density, radiance, halves, sems, out_sems):
-    def one_group(group, carry):
+def halves_kernel(density_in, radiance_in, near, far, density, radiance, held, sems, out_sems):
+    def one_group(out, first, group, carry):
         base = pl.multiple_of(group * GROUP, GROUP)
         here = sample_row(density, 0, 0, base)
         color = [sample_row(radiance, c, 0, base) for c in range(3)]
@@ -235,68 +230,84 @@
                 doubled = doubled + (here + nxt)
                 here, before, color = nxt, color, after
             for c in range(3):
-                halves[c * EIGHTS + i // 8, sample_place(i, base), :] = store[c]
+                out[c * EIGHTS + i // 8, sample_place(i, base - first), :] = store[c]
         return carry
 
     arrivals = fetches([(density_in, density), (radiance_in, radiance)], sems)
-    in_chunks(arrivals, fetches([(halves, out)], out_sems), TILES // GROUP, one_group)
+    departures = fetches([(held, far)], out_sems)
+    start_all(arrivals)
+    each = TILES // GROUP // len(arrivals)
+    kept = NEAR // GROUP // each
+    for k, some in enumerate(arrivals):
+        wait_all([some])
+        out, first = (near, 0) if k < kept else (held, NEAR)
+        lax.fori_loop(k * each, (k + 1) * each, functools.partial(one_group, out, first), 0)
+        if k >= kept:
+            start_all([departures[k - kept]])
+    wait_all(departures)
 
 
 def halves_of(density, radiance, chunks=8):
-    shape = (3 * EIGHTS, TILES * 8, LANES)
+    far = (3 * EIGHTS, (TILES - NEAR) * 8, LANES)
     return call(
         halves_kernel,
         "slab_halves",
         [FAR, FAR],
-        FAR,
-        jax.ShapeDtypeStruct(shape, F32),
+        [WHOLE, FAR],
+        [
+            jax.ShapeDtypeStruct((3 * EIGHTS, NEAR * 8, LANES), F32),
+            jax.ShapeDtypeStruct(far, F32),
+        ],
         [
             pltpu.VMEM((EIGHTS, TILES * 8, LANES), F32),
-            pltpu.VMEM(shape, F32),
-            pltpu.VMEM(shape, F32),
+            pltpu.VMEM((3 * EIGHTS, TILES * 8, LANES), F32),
+            pltpu.VMEM(far, F32),
             pltpu.SemaphoreType.DMA((chunks, 2)),
-            pltpu.SemaphoreType.DMA((chunks, 1)),
-        ],
-        LARGE,
+            pltpu.SemaphoreType.DMA((chunks * (TILES - NEAR) // TILES, 1)),
+        ],
+        HALVES_MIB,
         1_000_000_000,
     )(density, radiance)
 
 
-def loss_kernel(back, out):
-    total = back[0, LOSS : LOSS + OWNED, :]
-    for s in range(1, SLABS):
-        total = total + back[s, LOSS : LOSS + OWNED, :]
-    total = jnp.sum(total, axis=0, keepdims=True)
+def loss_kernel(back, near, out, near_out):
+    total = jnp.sum(back[pl.ds(LOSS, SLABS, stride=ANSWER), :], axis=0, keepdims=True)
     for z in range(out.shape[0]):
         out[z] = total
 
 
-def tile_loss(back, count):
-    return call(
+def tile_loss(back, near, count):
+    return pl.pallas_call(
         loss_kernel,
-        "tile_loss",
-        [WHOLE],
-        WHOLE,
-        jax.ShapeDtypeStruct((count, 1, LANES), F32),
-        [],
-        4,
-    )(back)
-
-
-def gradient_kernel(halves_in, back, out, halves, held, sems, out_sems):
+        in_specs=[WHOLE, WHOLE],
+        out_specs=[WHOLE, WHOLE],
+        out_shape=[
+            jax.ShapeDtypeStruct((count, 1, LANES), F32),
+            jax.ShapeDtypeStruct(near.shape, F32),
+        ],
+        input_output_aliases={1: 1},
+        compiler_params=pltpu.CompilerParams(vmem_limit_bytes=8 * MIB),
+        cost_estimate=pl.CostEstimate(flops=0, bytes_accessed=1024, transcendentals=0),
+        name="tile_loss",
+    )(back, near)
+
+
+def gradient_kernel(near, far_in, back, out, far, held, sems, out_sems):
     sample = lax.broadcasted_iota(jnp.int32, (8, LANES), 0)
 
-    def one_owner(owner, carry):
+    def one_owner(halves, first, owner, carry):
         for k in range(OWNED):
-            rows = pl.ds(pl.multiple_of(owner * (OWNED * 8), OWNED * 8) + k * 8, 8)
+            tile = owner * OWNED + k
+            rows = pl.ds(pl.multiple_of(tile * 8, 8), 8)
+            from_rows = pl.ds(pl.multiple_of((tile - first) * 8, 8), 8)
             known = [
-                jnp.broadcast_to(back[owner, q * OWNED + k : q * OWNED + k + 1, :], (8, LANES))
+                jnp.broadcast_to(back[pl.ds(owner * ANSWER + q * OWNED + k, 1), :], (8, LANES))
                 for q in range(6)
             ]
             for a in range(EIGHTS):
-                value = known[0] * halves[a, rows, :]
-                value += known[1] * halves[EIGHTS + a, rows, :]
-                value += known[2] * halves[2 * EIGHTS + a, rows, :]
+                value = known[0] * halves[a, from_rows, :]
+                value += known[1] * halves[EIGHTS + a, from_rows, :]
+                value += known[2] * halves[2 * EIGHTS + a, from_rows, :]
                 left = known[3]
                 if a == 0:
                     left = jnp.where(sample == 0, known[4], left)
@@ -305,39 +316,51 @@
                 held[a, rows, :] = value - left
         return carry
 
-    arrivals = fetches([(halves_in, halves)], sems)
-    in_chunks(arrivals, fetches([(held, out)], out_sems), SLABS, one_owner)
-
-
-def gradient(halves, back, chunks=8):
+    arrivals = fetches([(far_in, far)], sems)
+    departures = fetches([(held, out)], out_sems)
+    start_all(arrivals)
+    each = SLABS // len(departures)
+    kept = len(departures) - len(arrivals)
+    for k, some in enumerate(departures):
+        if k >= kept:
+            wait_all([arrivals[k - kept]])
+        halves, first = (near, 0) if k < kept else (far, NEAR)
+        lax.fori_loop(k * each, (k + 1) * each, functools.partial(one_owner, halves, first), 0)
+        start_all([some])
+    wait_all(departures)
+
+
+def gradient(near, far, back, chunks=8):
     shape = (EIGHTS, TILES * 8, LANES)
     return call(
         gradient_kernel,
         "slab_gradient",
-        [FAR, WHOLE],
+        [WHOLE, FAR, WHOLE],
         FAR,
         jax.ShapeDtypeStruct(shape, F32),
         [
-            pltpu.VMEM((3 * EIGHTS, TILES * 8, LANES), F32),
+            pltpu.VMEM((3 * EIGHTS, (TILES - NEAR) * 8, LANES), F32),
             pltpu.VMEM(shape, F32),
+            pltpu.SemaphoreType.DMA((chunks * (TILES - NEAR) // TILES, 1)),
             pltpu.SemaphoreType.DMA((chunks, 1)),
-            pltpu.SemaphoreType.DMA((chunks, 1)),
-        ],
-        LARGE,
+        ],
+        GRADIENT_MIB,
         1_000_000_000,
-    )(halves, back)
+    )(near, far, back)
 
 
 def on_device(density, radiance, target):
     density, radiance = tiled_view(density), tiled_view(radiance)
     owner = lax.axis_index("depth").astype(jnp.int32)[None]
-    slabs = lax.all_to_all(inner(density, radiance), "depth", 0, 0, tiled=True)
+    slabs = lax.all_to_all(inner(owner, density, radiance), "depth", 0, 0, tiled=True)
     answers = scan_slabs(owner, slabs, target)
-    back = lax.all_to_all(answers, "depth", 0, 0, tiled=True)
-    halves = halves_of(density, radiance)
+    answers = answers.reshape(SLABS, ANSWER, 1, LANES)
+    back = lax.all_to_all(answers, "depth", 0, 0, tiled=True).reshape(SLABS * ANSWER, LANES)
+    near, far = halves_of(density, radiance)
     zs = lax.axis_size("rays")
-    losses = lax.all_to_all(tile_loss(back, zs), "rays", 0, 0, tiled=True)
-    grad = gradient(halves, back)
+    tile, near = tile_loss(back, near, zs)
+    losses = lax.all_to_all(tile, "rays", 0, 0, tiled=True)
+    grad = gradient(near, far, back)
     loss_mean = jnp.sum(losses) / (3.0 * zs * TILES * LANES)
     return untiled_view(grad), loss_mean
 

time: 62.9 us -> 60.4 us (0.960)
  blocking collectives: 0 us -> 22.6 us
  waiting for transfers between devices: 21 us -> 7.63 us
  starting transfers between devices: 20.6 us -> 12 us
  Pallas kernels: 17.9 us -> 13.2 us
  local copies, waits for them, and re-layouts: 0.01 us -> 1.59 us
    all_to_all x0 -> x1, blocking collectives: none -> 22.6 us  [on_device(): lax.all_to_all(inner(owner, density, radiance), 'depth', 0, 0, tiled=True)]
    all_to_all x3 -> x2, waiting for transfers between devices: 21 us -> 7.63 us  [the longest x1 4.36 us: on_device(): lax.all_to_all(answers, 'depth', 0, 0, tiled=True)]
    all_to_all x3 -> x2, starting transfers between devices: 20.6 us -> 12 us  [the longest x1 8.19 us: on_device(): losses = lax.all_to_all(tile, 'rays', 0, 0, tiled=True)]
    pallas_call x4, Pallas kernels: 16.8 us -> 12.1 us  [the longest x1 4.48 us: halves_of(): call(halves_kernel, 'slab_halves', [FAR, FAR], [WHOLE, FAR], [jax.ShapeDt...]
    unnamed x4, local copies, waits for them, and re-layouts: 0.01 us -> 1.59 us
  transfers between devices with their start and end apart: 3 -> 2, of which waited for: 3 -> 2; matrix products, arithmetic and copies ran while one was open for 0% -> 0% of each run, Pallas kernels for 18% -> 13%
where the time goes in v2:
time: 60.4 us; the launch traced here: 60.1 us
  blocking collectives  22.6 us (37%)
  Pallas kernels  13.2 us (22%)
  starting transfers between devices  12 us (20%)
  waiting for transfers between devices  7.63 us (13%)
  between operations  2.46 us (4%)
  local copies, waits for them, and re-layouts  1.59 us (3%)
  other arithmetic  0.61 us (1%)
    all_to_all x1, blocking collectives, on_device(): lax.all_to_all(inner(owner, density, radiance), 'depth', 0, 0, tiled=True)  22.6 us
    all_to_all x1, starting transfers between devices, on_device(): losses = lax.all_to_all(tile, 'rays', 0, 0, tiled=True)  8.19 us
    pallas_call x1, Pallas kernels, halves_of(): call(halves_kernel, 'slab_halves', [FAR, FAR], [WHOLE, FAR], [jax.ShapeDt...  4.48 us
    all_to_all x1, waiting for transfers between devices, on_device(): lax.all_to_all(answers, 'depth', 0, 0, tiled=True)  4.36 us
    all_to_all x1, starting transfers between devices, on_device(): lax.all_to_all(answers, 'depth', 0, 0, tiled=True)  3.79 us
    pallas_call x1, Pallas kernels, inner(): call(inner_kernel, 'slab_inner', [pl.BlockSpec(memory_space=pltpu.SMEM),...  3.79 us
    pallas_call x1, Pallas kernels, gradient(): call(gradient_kernel, 'slab_gradient', [WHOLE, FAR, WHOLE], FAR, jax.Shap...  3.27 us
    all_to_all x1, waiting for transfers between devices, on_device(): losses = lax.all_to_all(tile, 'rays', 0, 0, tiled=True)  3.27 us
  transfers between devices with their start and end apart: 2, of which 2 were waited for; matrix products, arithmetic and copies ran while one was open for 0% of the time, Pallas kernels for 13%

profile of v2, /device:TPU:1, one launch (start us, length us, event | category | flops | bytes accessed | tf_op | source)
XLA Modules:
  0.0 60.1 jit_solution(8984962889390614454)
XLA Ops:
  0.6 0.0 copy-start.1
  0.6 3.8 %slab_inner.1 = f32[32,48,128]{2,1,0:T(8,128)S(1)} custom-call(s32[1]{0:T(128)} %bitcast.owner, f32[4,1024,128]{2,1,0:T(8,128)} %bitcast.18, f32[12,1024,128]{2,1,0:T(8,128)} %bitcast.22), custom_call_target="tpu_custom_call" | custom-call | bytes 1024 | tf_op jit(solution)/shard_map/slab_inner/pallas_call | solution.py:129
  4.4 22.6 %all_to_all.15.slabs = f32[32,48,128]{2,1,0:T(8,128)S(1)} all-to-all(f32[32,48,128]{2,1,0:T(8,128)S(1)} %slab_inner.1), channel_id=1, replica_groups=mesh['depth'=32,'rays'=8] {'depth'}, dimensions={0} | all-to-all | bytes 1572864 | tf_op jit(solution)/shard_map/all_to_all | solution.py:355
  27.1 0.0 copy-done.1
  27.1 1.1 %scan_slabs.1 = f32[800,128]{1,0:T(8,128)} custom-call(s32[1]{0:T(128)} %bitcast.owner, f32[32,48,128]{2,1,0:T(8,128)S(1)} %all_to_all.15.slabs, f32[3,16384]{1,0:T(4,128)S(1)} %copy-done.1), custom_call_target="tpu_custom_call" | custom-call | bytes 1024 | tf_op jit(solution)/shard_map/scan_slabs/pallas_call | solution.py:198
  28.1 3.8 %all-to-all-start.1 = ((f32[32,25,1,128]{3,2,1,0:T(1,128)}), f32[32,25,1,128]{3,2,1,0:T(1,128)S(1)}, u32[]{:S(2)}, u32[]{:S(2)}) async-start(f32[32,25,1,128]{3,2,1,0:T(1,128)} %bitcast.7), calls=%async_computation.1 | async-start | bytes 819200 | tf_op jit(solution)/shard_map/all_to_all | solution.py:358
  31.9 0.0 copy-start
  32.0 1.6 %copy-done = f32[32,16384]{1,0:T(8,128)S(1)} copy-done((f32[32,16384]{1,0:T(8,128)S(1)}, f32[32,16384]{1,0:T(8,128)}, u32[]{:S(2)}) %copy-start) | copy-done | bytes 2097176
  33.5 4.5 %slab_halves.1 = (f32[12,384,128]{2,1,0:T(8,128)S(1)}, f32[12,640,128]{2,1,0:T(8,128)}) custom-call(f32[4,1024,128]{2,1,0:T(8,128)S(1)} %bitcast.19, f32[12,1024,128]{2,1,0:T(8,128)} %bitcast.23), custom_call_target="tpu_custom_call" | custom-call | flops 1000000000 | bytes 1024 | tf_op jit(solution)/shard_map/slab_halves/pallas_call | solution.py:252
  38.0 4.4 %all-to-all-done.1 = f32[32,25,1,128]{3,2,1,0:T(1,128)S(1)} async-done(((f32[32,25,1,128]{3,2,1,0:T(1,128)}), f32[32,25,1,128]{3,2,1,0:T(1,128)S(1)}, u32[]{:S(2)}, u32[]{:S(2)}) %all-to-all-start.1) | async-done | bytes 409632 | tf_op jit(solution)/shard_map/all_to_all | solution.py:358
  42.4 0.6 %tile_loss.1 = (f32[8,1,128]{2,1,0:T(1,128)}, f32[12,384,128]{2,1,0:T(8,128)S(1)}) custom-call(f32[800,128]{1,0:T(8,128)S(1)} %bitcast.20, f32[12,384,128]{2,1,0:T(8,128)S(1)} %get-tuple-element.6.near), custom_call_target="tpu_custom_call", output_to_operand_aliasing={{1}: (1, {})} | custom-call | bytes 1024 | tf_op jit(solution)/shard_map/tile_loss/pallas_call | solution.py:280
  43.0 8.2 %all-to-all-start.2 = ((f32[8,1,128]{2,1,0:T(1,128)}), f32[8,1,128]{2,1,0:T(1,128)S(1)}, u32[]{:S(2)}, u32[]{:S(2)}) async-start(f32[8,1,128]{2,1,0:T(1,128)} %get-tuple-element.9), calls=%async_computation.2 | async-start | bytes 8192 | tf_op jit(solution)/shard_map/all_to_all | solution.py:362
  51.2 3.3 %slab_gradient.1 = f32[4,1024,128]{2,1,0:T(8,128)} custom-call(f32[12,384,128]{2,1,0:T(8,128)S(1)} %get-tuple-element.7.near, f32[12,640,128]{2,1,0:T(8,128)} %get-tuple-element.8.far_in, f32[800,128]{1,0:T(8,128)S(1)} %bitcast.21), custom_call_target="tpu_custom_call" | custom-call | flops 1000000000 | bytes 1024 | tf_op jit(solution)/shard_map/slab_gradient/pallas_call | solution.py:335
  54.5 3.3 %all-to-all-done.2 = f32[8,1,128]{2,1,0:T(1,128)S(1)} async-done(((f32[8,1,128]{2,1,0:T(1,128)}), f32[8,1,128]{2,1,0:T(1,128)S(1)}, u32[]{:S(2)}, u32[]{:S(2)}) %all-to-all-start.2) | async-done | bytes 4128 | tf_op jit(solution)/shard_map/all_to_all | solution.py:362
  57.7 0.6 %reduce_sum.9 = f32[]{:T(128)} reduce(f32[8,1,128]{2,1,0:T(1,128)S(1)} %all-to-all-done.2, f32[]{:T(128)} %constant.9.clone.1), dimensions={0,1,2}, to_apply=%region_0.0 | reduce | flops 1023 | bytes 4104 | tf_op jit(solution)/shard_map/reduce_sum | solution.py:364
Async XLA Ops:
  0.6 26.4 %copy-start.1 = (f32[3,16384]{1,0:T(4,128)S(1)}, f32[3,16384]{1,0:T(4,128)}, u32[]{:S(2)}) copy-start(f32[3,16384]{1,0:T(4,128)} %target.1) | copy-start | bytes 589828
  28.1 14.2 %all-to-all-start.1 = ((f32[32,25,1,128]{3,2,1,0:T(1,128)}), f32[32,25,1,128]{3,2,1,0:T(1,128)S(1)}, u32[]{:S(2)}, u32[]{:S(2)}) async-start(f32[32,25,1,128]{3,2,1,0:T(1,128)} %bitcast.7), calls=%async_computation.1 | async-start | bytes 819200 | tf_op jit(solution)/shard_map/all_to_all | solution.py:358
  31.9 1.6 %copy-start = (f32[32,16384]{1,0:T(8,128)S(1)}, f32[32,16384]{1,0:T(8,128)}, u32[]{:S(2)}) copy-start(f32[32,16384]{1,0:T(8,128)} %param.3) | copy-start | bytes 6291460
  43.0 14.7 %all-to-all-start.2 = ((f32[8,1,128]{2,1,0:T(1,128)}), f32[8,1,128]{2,1,0:T(1,128)S(1)}, u32[]{:S(2)}, u32[]{:S(2)}) async-start(f32[8,1,128]{2,1,0:T(1,128)} %get-tuple-element.9), calls=%async_computation.2 | async-start | bytes 8192 | tf_op jit(solution)/shard_map/all_to_all | solution.py:362

commit v3 on v2

--- a/solution.py
+++ b/solution.py
@@ -14,12 +14,13 @@
 LANES = 128
 OWNED = TILES // SLABS
 GROUP = 8
-SENT = 12
-LOSS = 6 * OWNED
+KNOWN = 12
+SENT = 8
+LOSS = 5 * OWNED
 ANSWER = LOSS + 1
 F32 = jnp.float32
 MIB = 1 << 20
-INNER_MIB, HALVES_MIB, GRADIENT_MIB = 52, 49.5, 50
+INNER_MIB, HALVES_MIB, GRADIENT_MIB = 52, 48, 50
 NEAR = 48
 WHOLE = pl.BlockSpec(memory_space=pltpu.VMEM)
 FAR = pl.BlockSpec(memory_space=pltpu.HBM)
@@ -93,7 +94,8 @@
         wait_all(departures)
 
 
-def inner_kernel(owner, density_in, radiance_in, sent, density, radiance, sems):
+def inner_kernel(slab, density_in, radiance_in, out, edge, density, radiance, sems):
+    odd = slab[0] % 2 == 1
     def one_group(group, carry):
         base = pl.multiple_of(group * GROUP, GROUP)
         first = here = sample_row(density, 0, 0, base)
@@ -113,32 +115,74 @@
             half = 0.5 * jnp.exp(-0.5 * doubled)
             before, color, here = color, after, nxt
         known = [total[c] - half * before[c] for c in range(3)]
-        parts = [doubled, here, first] + known + color + first_color
-        for q in range(SENT):
-            for k in range(GROUP // OWNED):
-                owner = group * (GROUP // OWNED) + k
-                sent[owner, q * OWNED : (q + 1) * OWNED, :] = parts[q][k * OWNED : (k + 1) * OWNED, :]
+        rows = pl.ds(base, GROUP)
+        for q, part in enumerate([doubled, here, first] + known + color + first_color):
+            out[q, rows, :] = part
+        edge[0, rows, :] = first
+        for c in range(3):
+            edge[1 + c, rows, :] = jnp.where(odd, first_color[c], color[c])
         return carry
 
     arrivals = fetches([(density_in, density), (radiance_in, radiance)], sems)
     in_chunks(arrivals, None, TILES // GROUP, one_group)
 
 
-def inner(owner, density, radiance, chunks=8):
-    shape = (SLABS, SENT * OWNED, LANES)
+def inner(slab, density, radiance, chunks=8):
     return call(
         inner_kernel,
         "slab_inner",
         [pl.BlockSpec(memory_space=pltpu.SMEM), FAR, FAR],
-        WHOLE,
-        jax.ShapeDtypeStruct(shape, F32),
+        [WHOLE, WHOLE],
+        [
+            jax.ShapeDtypeStruct((KNOWN, TILES, LANES), F32),
+            jax.ShapeDtypeStruct((4, TILES, LANES), F32),
+        ],
         [
             pltpu.VMEM((EIGHTS, TILES * 8, LANES), F32),
             pltpu.VMEM((3 * EIGHTS, TILES * 8, LANES), F32),
             pltpu.SemaphoreType.DMA((chunks, 2)),
         ],
         INNER_MIB,
-    )(owner, density, radiance)
+    )(slab, density, radiance)
+
+
+def closing_kernel(slab, known, rim, out):
+    def send(parity, parts_of):
+        @pl.when(slab[0] % 2 == parity)
+        def _():
+            for group in range(TILES // GROUP):
+                rows = pl.ds(group * GROUP, GROUP)
+                for q, part in enumerate(parts_of(rows)):
+                    for k in range(GROUP // OWNED):
+                        owner = group * (GROUP // OWNED) + k
+                        out[owner, q * OWNED : (q + 1) * OWNED, :] = part[k * OWNED : (k + 1) * OWNED, :]
+
+    def even(rows):
+        part = [known[q, rows, :] for q in range(KNOWN)]
+        after = [rim[1 + c, rows, :] for c in range(3)]
+        depth = 0.5 * (part[0] + part[1] + rim[0, rows, :])
+        half = 0.5 * jnp.exp(-0.5 * part[0])
+        behind = 0.5 * jnp.exp(-depth)
+        color = [part[3 + c] + half * after[c] - behind * (part[6 + c] + after[c]) for c in range(3)]
+        return [depth] + color + [part[2]] + part[9:]
+
+    def odd(rows):
+        return [known[q, rows, :] for q in (0, 3, 4, 5, 1, 6, 7, 8)]
+
+    send(0, even)
+    send(1, odd)
+
+
+def closing(slab, known, rim):
+    return call(
+        closing_kernel,
+        "slab_closing",
+        [pl.BlockSpec(memory_space=pltpu.SMEM), WHOLE, WHOLE],
+        WHOLE,
+        jax.ShapeDtypeStruct((SLABS, SENT * OWNED, LANES), F32),
+        [],
+        6,
+    )(slab, known, rim)
 
 
 def scan_kernel(owner, slabs, target, out):
@@ -150,23 +194,23 @@
     pixel = [zero] * 3
     offsets, befores, ends = [], [], []
     for s in range(SLABS):
-        more = s < SLABS - 1
-        doubled = value(s, 0)
-        depth = 0.5 * (doubled + value(s, 1) + (value(s + 1, 2) if more else zero))
-        half = 0.5 * jnp.exp(-0.5 * doubled)
-        behind = 0.5 * jnp.exp(-depth)
         offset = jnp.exp(-start)
-        end = []
+        offsets.append(offset)
         befores.append(pixel)
-        following = []
-        for c in range(3):
-            after = value(s + 1, 9 + c) if more else zero
-            last = value(s, 3 + c) + half * after
-            end.append(offset * last)
-            following.append(pixel[c] + offset * (last - behind * (value(s, 6 + c) + after)))
-        pixel = following
-        offsets.append(offset)
-        ends.append(end)
+        color = [value(s, 1 + c) for c in range(3)]
+        if s % 2 == 0:
+            depth = value(s, 0)
+            ends.append(None)
+        else:
+            more = s < SLABS - 1
+            depth = 0.5 * (value(s, 0) + value(s, 4) + (value(s + 1, 4) if more else zero))
+            half = 0.5 * jnp.exp(-0.5 * value(s, 0))
+            behind = 0.5 * jnp.exp(-depth)
+            after = [value(s + 1, 5 + c) if more else zero for c in range(3)]
+            color = [color[c] + half * after[c] for c in range(3)]
+            ends.append([offset * color[c] for c in range(3)])
+            color = [color[c] - behind * (value(s, 5 + c) + after[c]) for c in range(3)]
+        pixel = [pixel[c] + offset * color[c] for c in range(3)]
         start = start + depth
     first = owner[0] * (OWNED * LANES)
     error = []
@@ -183,15 +227,17 @@
     for s in range(SLABS):
         left = [residual[c] * (pixel[c] - befores[s][c]) for c in range(3)]
         left = left[0] + left[1] + left[2]
-        last = [residual[c] * ends[s][c] for c in range(3)]
-        last = last[0] + last[1] + last[2] - left
-        answer = [offsets[s] * residual[c] for c in range(3)]
-        answer += [left, 0.5 * (left - previous), 0.5 * (left - last)]
+        answer = [offsets[s] * residual[c] for c in range(3)] + [left]
+        if s % 2 == 0:
+            answer += [0.5 * (left - previous)]
+        else:
+            last = [residual[c] * ends[s][c] for c in range(3)]
+            previous = last[0] + last[1] + last[2] - left
+            answer += [0.5 * (left - previous)]
         top = s * ANSWER
         for q, part in enumerate(answer):
             out[top + q * OWNED : top + (q + 1) * OWNED, :] = part
         out[top + LOSS : top + ANSWER, :] = loss
-        previous = last
 
 
 def scan_slabs(owner, slabs, target):
@@ -206,31 +252,38 @@
     )(owner, slabs, target)
 
 
-def halves_kernel(density_in, radiance_in, near, far, density, radiance, held, sems, out_sems):
+def halves_kernel(slab, density_in, radiance_in, rim, near, far, density, radiance, held, sems, out_sems):
+    even = slab[0] % 2 == 0
+    odd_share = jnp.where(even, 0.0, 0.25)
+
     def one_group(out, first, group, carry):
         base = pl.multiple_of(group * GROUP, GROUP)
         here = sample_row(density, 0, 0, base)
+        rows = pl.ds(base, GROUP)
         color = [sample_row(radiance, c, 0, base) for c in range(3)]
+        beside = [rim[1 + c, rows, :] for c in range(3)]
         before = color
         doubled = jnp.zeros((GROUP, LANES), F32)
         half = None
         for i in range(SAMPLES):
-            store = half
-            if i < SAMPLES - 1:
-                after = [sample_row(radiance, c, i + 1, base) for c in range(3)]
-                if i == 0:
-                    half = [0.25 * (color[c] + after[c]) for c in range(3)]
-                    store = half
-                else:
-                    transmit = 0.25 * jnp.exp(-0.5 * doubled)
-                    new = [half[c] + transmit * (after[c] - before[c]) for c in range(3)]
-                    store = [half[c] + new[c] for c in range(3)]
-                    half = new
+            last = i == SAMPLES - 1
+            after = beside if last else [sample_row(radiance, c, i + 1, base) for c in range(3)]
+            if i == 0:
+                new = [0.25 * (color[c] + after[c]) for c in range(3)]
+                store = [new[c] + odd_share * (beside[c] + color[c]) for c in range(3)]
+            else:
+                transmit = 0.25 * jnp.exp(-0.5 * doubled)
+                new = [half[c] + transmit * (after[c] - before[c]) for c in range(3)]
+                if last:
+                    new = [jnp.where(even, new[c], 0.0) for c in range(3)]
+                store = [half[c] + new[c] for c in range(3)]
+            for c in range(3):
+                out[c * EIGHTS + i // 8, sample_place(i, base - first), :] = store[c]
+            if not last:
                 nxt = sample_row(density, 0, i + 1, base)
                 doubled = doubled + (here + nxt)
-                here, before, color = nxt, color, after
-            for c in range(3):
-                out[c * EIGHTS + i // 8, sample_place(i, base - first), :] = store[c]
+                here = nxt
+            before, color, half = color, after, new
         return carry
 
     arrivals = fetches([(density_in, density), (radiance_in, radiance)], sems)
@@ -247,12 +300,12 @@
     wait_all(departures)
 
 
-def halves_of(density, radiance, chunks=8):
+def halves_of(slab, density, radiance, rim, chunks=8):
     far = (3 * EIGHTS, (TILES - NEAR) * 8, LANES)
     return call(
         halves_kernel,
         "slab_halves",
-        [FAR, FAR],
+        [pl.BlockSpec(memory_space=pltpu.SMEM), FAR, FAR, WHOLE],
         [WHOLE, FAR],
         [
             jax.ShapeDtypeStruct((3 * EIGHTS, NEAR * 8, LANES), F32),
@@ -267,7 +320,7 @@
         ],
         HALVES_MIB,
         1_000_000_000,
-    )(density, radiance)
+    )(slab, density, radiance, rim)
 
 
 def loss_kernel(back, near, out, near_out):
@@ -292,8 +345,11 @@
     )(back, near)
 
 
-def gradient_kernel(near, far_in, back, out, far, held, sems, out_sems):
+def gradient_kernel(slab, near, far_in, back, out, far, held, sems, out_sems):
     sample = lax.broadcasted_iota(jnp.int32, (8, LANES), 0)
+    even = slab[0] % 2 == 0
+    top = sample == jnp.where(even, 0, 8)
+    bottom = sample == jnp.where(even, 8, 7)
 
     def one_owner(halves, first, owner, carry):
         for k in range(OWNED):
@@ -302,7 +358,7 @@
             from_rows = pl.ds(pl.multiple_of((tile - first) * 8, 8), 8)
             known = [
                 jnp.broadcast_to(back[pl.ds(owner * ANSWER + q * OWNED + k, 1), :], (8, LANES))
-                for q in range(6)
+                for q in range(5)
             ]
             for a in range(EIGHTS):
                 value = known[0] * halves[a, from_rows, :]
@@ -310,9 +366,9 @@
                 value += known[2] * halves[2 * EIGHTS + a, from_rows, :]
                 left = known[3]
                 if a == 0:
-                    left = jnp.where(sample == 0, known[4], left)
+                    left = jnp.where(top, known[4], left)
                 if a == EIGHTS - 1:
-                    left = jnp.where(sample == 7, known[5], left)
+                    left = jnp.where(bottom, known[4], left)
                 held[a, rows, :] = value - left
         return carry
 
@@ -330,12 +386,12 @@
     wait_all(departures)
 
 
-def gradient(near, far, back, chunks=8):
+def gradient(slab, near, far, back, chunks=8):
     shape = (EIGHTS, TILES * 8, LANES)
     return call(
         gradient_kernel,
         "slab_gradient",
-        [WHOLE, FAR, WHOLE],
+        [pl.BlockSpec(memory_space=pltpu.SMEM), WHOLE, FAR, WHOLE],
         FAR,
         jax.ShapeDtypeStruct(shape, F32),
         [
@@ -346,21 +402,23 @@
         ],
         GRADIENT_MIB,
         1_000_000_000,
-    )(near, far, back)
+    )(slab, near, far, back)
 
 
 def on_device(density, radiance, target):
     density, radiance = tiled_view(density), tiled_view(radiance)
     owner = lax.axis_index("depth").astype(jnp.int32)[None]
-    slabs = lax.all_to_all(inner(owner, density, radiance), "depth", 0, 0, tiled=True)
+    known, edge = inner(owner, density, radiance)
+    rim = lax.ppermute(edge, "depth", [(s, s ^ 1) for s in range(SLABS)])
+    slabs = lax.all_to_all(closing(owner, known, rim), "depth", 0, 0, tiled=True)
     answers = scan_slabs(owner, slabs, target)
     answers = answers.reshape(SLABS, ANSWER, 1, LANES)
     back = lax.all_to_all(answers, "depth", 0, 0, tiled=True).reshape(SLABS * ANSWER, LANES)
-    near, far = halves_of(density, radiance)
+    near, far = halves_of(owner, density, radiance, rim)
     zs = lax.axis_size("rays")
     tile, near = tile_loss(back, near, zs)
     losses = lax.all_to_all(tile, "rays", 0, 0, tiled=True)
-    grad = gradient(near, far, back)
+    grad = gradient(owner, near, far, back)
     loss_mean = jnp.sum(losses) / (3.0 * zs * TILES * LANES)
     return untiled_view(grad), loss_mean
 

time: 60.4 us -> 58.5 us (0.969)
  blocking collectives: 22.6 us -> 17.2 us
  starting transfers between devices: 12 us -> 15.1 us
    all_to_all x1, blocking collectives: 22.6 us -> 17.2 us  [on_device(): lax.all_to_all(closing(owner, known, rim), 'depth', 0, 0, tiled=True)]
    ppermute x0 -> x1, starting transfers between devices: none -> 3.29 us  [on_device(): rim = lax.ppermute(edge, 'depth', [(s, s ^ 1) for s in range(SLABS)])]
    ppermute x0 -> x1, waiting for transfers between devices: none -> 1.16 us  [on_device(): rim = lax.ppermute(edge, 'depth', [(s, s ^ 1) for s in range(SLABS)])]
    all_to_all x1, waiting for transfers between devices: 4.36 us -> 3.59 us  [on_device(): lax.all_to_all(answers, 'depth', 0, 0, tiled=True)]
    pallas_call x2 -> x3, Pallas kernels: 7.75 us -> 7.89 us  [the longest x1 4.55 us: halves_of(): call(halves_kernel, 'slab_halves', [pl.BlockSpec(memory_space=pltpu.SMEM)...]
  transfers between devices with their start and end apart: 2 -> 3, of which waited for: 2 -> 3; matrix products, arithmetic and copies ran while one was open for 0% -> 0% of each run, Pallas kernels for 13% -> 13%
where the time goes in v3:
time: 58.5 us; the launch traced here: 58.2 us
  blocking collectives  17.2 us (29%)
  starting transfers between devices  15.1 us (26%)
  Pallas kernels  13.2 us (23%)
  waiting for transfers between devices  8.03 us (14%)
  between operations  2.47 us (4%)
  local copies, waits for them, and re-layouts  1.59 us (3%)
  other arithmetic  0.61 us (1%)
    all_to_all x1, blocking collectives, on_device(): lax.all_to_all(closing(owner, known, rim), 'depth', 0, 0, tiled=True)  17.2 us
    all_to_all x1, starting transfers between devices, on_device(): losses = lax.all_to_all(tile, 'rays', 0, 0, tiled=True)  8.19 us
    pallas_call x1, Pallas kernels, halves_of(): call(halves_kernel, 'slab_halves', [pl.BlockSpec(memory_space=pltpu.SMEM)...  4.55 us
    pallas_call x1, Pallas kernels, inner(): call(inner_kernel, 'slab_inner', [pl.BlockSpec(memory_space=pltpu.SMEM),...  3.76 us
    all_to_all x1, starting transfers between devices, on_device(): lax.all_to_all(answers, 'depth', 0, 0, tiled=True)  3.66 us
    all_to_all x1, waiting for transfers between devices, on_device(): lax.all_to_all(answers, 'depth', 0, 0, tiled=True)  3.59 us
    ppermute x1, starting transfers between devices, on_device(): rim = lax.ppermute(edge, 'depth', [(s, s ^ 1) for s in range(SLABS)])  3.29 us
    all_to_all x1, waiting for transfers between devices, on_device(): losses = lax.all_to_all(tile, 'rays', 0, 0, tiled=True)  3.28 us
  transfers between devices with their start and end apart: 3, of which 3 were waited for; matrix products, arithmetic and copies ran while one was open for 0% of the time, Pallas kernels for 13%

profile of v3, /device:TPU:1, one launch (start us, length us, event | category | flops | bytes accessed | tf_op | source)
XLA Modules:
  0.0 58.2 jit_solution(10514373384456993785)
XLA Ops:
  0.6 3.8 %slab_inner.1 = (f32[12,128,128]{2,1,0:T(8,128)S(1)}, f32[4,128,128]{2,1,0:T(8,128)S(1)}) custom-call(s32[1]{0:T(128)} %bitcast.slab.owner, f32[4,1024,128]{2,1,0:T(8,128)} %bitcast.18, f32[12,1024,128]{2,1,0:T(8,128)} %bitcast.22), custom_call_target="tpu_custom_call" | custom-call | bytes 1024 | tf_op jit(solution)/shard_map/slab_inner/pallas_call | solution.py:131
  4.4 0.0 copy-start.1
  4.4 3.3 %collective-permute-start = (f32[4,128,128]{2,1,0:T(8,128)S(1)}, f32[4,128,128]{2,1,0:T(8,128)S(1)}, u32[]{:S(2)}, u32[]{:S(2)}) collective-permute-start(f32[4,128,128]{2,1,0:T(8,128)S(1)} %get-tuple-element.9), channel_id=1, source_target_pairs={{0,8},{8,0},{16,24},{24,16},{32,40},{40,32},{48,56},{56,48},{64,72... | collective-permute-start | bytes 786440 | tf_op jit(solution)/shard_map/ppermute | solution.py:412
  7.7 1.2 %collective-permute-done.rim = f32[4,128,128]{2,1,0:T(8,128)S(1)} collective-permute-done((f32[4,128,128]{2,1,0:T(8,128)S(1)}, f32[4,128,128]{2,1,0:T(8,128)S(1)}, u32[]{:S(2)}, u32[]{:S(2)}) %collective-permute-start) | collective-permute-done | bytes 262176 | tf_op jit(solution)/shard_map/ppermute | solution.py:412
  8.9 0.1 slab_closing.1
  8.9 17.2 %all_to_all.15.slabs = f32[32,32,128]{2,1,0:T(8,128)S(1)} all-to-all(f32[32,32,128]{2,1,0:T(8,128)S(1)} %slab_closing.1), channel_id=1, replica_groups=mesh['depth'=32,'rays'=8] {'depth'}, dimensions={0} | all-to-all | bytes 1048576 | tf_op jit(solution)/shard_map/all_to_all | solution.py:413
  26.1 0.0 copy-done.1
  26.1 1.0 %scan_slabs.1 = f32[672,128]{1,0:T(8,128)} custom-call(s32[1]{0:T(128)} %bitcast.slab.owner, f32[32,32,128]{2,1,0:T(8,128)S(1)} %all_to_all.15.slabs, f32[3,16384]{1,0:T(4,128)S(1)} %copy-done.1), custom_call_target="tpu_custom_call" | custom-call | bytes 1024 | tf_op jit(solution)/shard_map/scan_slabs/pallas_call | solution.py:244
  27.1 3.7 %all-to-all-start.1 = ((f32[32,21,1,128]{3,2,1,0:T(1,128)}), f32[32,21,1,128]{3,2,1,0:T(1,128)S(1)}, u32[]{:S(2)}, u32[]{:S(2)}) async-start(f32[32,21,1,128]{3,2,1,0:T(1,128)} %bitcast.7), calls=%async_computation.1 | async-start | bytes 688128 | tf_op jit(solution)/shard_map/all_to_all | solution.py:416
  30.8 0.0 copy-start
  30.8 1.6 %copy-done = f32[32,16384]{1,0:T(8,128)S(1)} copy-done((f32[32,16384]{1,0:T(8,128)S(1)}, f32[32,16384]{1,0:T(8,128)}, u32[]{:S(2)}) %copy-start) | copy-done | bytes 2097176
  32.4 4.5 %slab_halves.1 = (f32[12,384,128]{2,1,0:T(8,128)S(1)}, f32[12,640,128]{2,1,0:T(8,128)}) custom-call(s32[1]{0:T(128)} %bitcast.slab.owner, f32[4,1024,128]{2,1,0:T(8,128)S(1)} %bitcast.19, f32[12,1024,128]{2,1,0:T(8,128)} %bitcast.23, f32[4,128,128]{2,1,0:T(8,128)S(1)} %collective-permute-done.rim), custom_call_target="tpu_custom_call" | custom-call | flops 1000000000 | bytes 1024 | tf_op jit(solution)/shard_map/slab_halves/pallas_call | solution.py:305
  36.9 3.6 %all-to-all-done.1 = f32[32,21,1,128]{3,2,1,0:T(1,128)S(1)} async-done(((f32[32,21,1,128]{3,2,1,0:T(1,128)}), f32[32,21,1,128]{3,2,1,0:T(1,128)S(1)}, u32[]{:S(2)}, u32[]{:S(2)}) %all-to-all-start.1) | async-done | bytes 344096 | tf_op jit(solution)/shard_map/all_to_all | solution.py:416
  40.5 0.6 %tile_loss.1 = (f32[8,1,128]{2,1,0:T(1,128)}, f32[12,384,128]{2,1,0:T(8,128)S(1)}) custom-call(f32[672,128]{1,0:T(8,128)S(1)} %bitcast.20, f32[12,384,128]{2,1,0:T(8,128)S(1)} %get-tuple-element.10.near), custom_call_target="tpu_custom_call", output_to_operand_aliasing={{1}: (1, {})} | custom-call | bytes 1024 | tf_op jit(solution)/shard_map/tile_loss/pallas_call | solution.py:333
  41.1 8.2 %all-to-all-start.2 = ((f32[8,1,128]{2,1,0:T(1,128)}), f32[8,1,128]{2,1,0:T(1,128)S(1)}, u32[]{:S(2)}, u32[]{:S(2)}) async-start(f32[8,1,128]{2,1,0:T(1,128)} %get-tuple-element.13), calls=%async_computation.2 | async-start | bytes 8192 | tf_op jit(solution)/shard_map/all_to_all | solution.py:420
  49.3 3.3 %slab_gradient.1 = f32[4,1024,128]{2,1,0:T(8,128)} custom-call(s32[1]{0:T(128)} %bitcast.slab.owner, f32[12,384,128]{2,1,0:T(8,128)S(1)} %get-tuple-element.11.near, f32[12,640,128]{2,1,0:T(8,128)} %get-tuple-element.12.far_in, f32[672,128]{1,0:T(8,128)S(1)} %bitcast.21), custom_call_target="tpu_custom_call" | custom-call | flops 1000000000 | bytes 1024 | tf_op jit(solution)/shard_map/slab_gradient/pallas_call | solution.py:391
  52.6 3.3 %all-to-all-done.2 = f32[8,1,128]{2,1,0:T(1,128)S(1)} async-done(((f32[8,1,128]{2,1,0:T(1,128)}), f32[8,1,128]{2,1,0:T(1,128)S(1)}, u32[]{:S(2)}, u32[]{:S(2)}) %all-to-all-start.2) | async-done | bytes 4128 | tf_op jit(solution)/shard_map/all_to_all | solution.py:420
  55.8 0.6 %reduce_sum.9 = f32[]{:T(128)} reduce(f32[8,1,128]{2,1,0:T(1,128)S(1)} %all-to-all-done.2, f32[]{:T(128)} %constant.9.clone.1), dimensions={0,1,2}, to_apply=%region_0.0 | reduce | flops 1023 | bytes 4104 | tf_op jit(solution)/shard_map/reduce_sum | solution.py:422
Async XLA Ops:
  4.4 21.7 %copy-start.1 = (f32[3,16384]{1,0:T(4,128)S(1)}, f32[3,16384]{1,0:T(4,128)}, u32[]{:S(2)}) copy-start(f32[3,16384]{1,0:T(4,128)} %target.1) | copy-start | bytes 589828
  4.4 4.5 %collective-permute-start = (f32[4,128,128]{2,1,0:T(8,128)S(1)}, f32[4,128,128]{2,1,0:T(8,128)S(1)}, u32[]{:S(2)}, u32[]{:S(2)}) collective-permute-start(f32[4,128,128]{2,1,0:T(8,128)S(1)} %get-tuple-element.9), channel_id=1, source_target_pairs={{0,8},{8,0},{16,24},{24,16},{32,40},{40,32},{48,56},{56,48},{64,72... | collective-permute-start | bytes 786440 | tf_op jit(solution)/shard_map/ppermute | solution.py:412
  27.1 13.4 %all-to-all-start.1 = ((f32[32,21,1,128]{3,2,1,0:T(1,128)}), f32[32,21,1,128]{3,2,1,0:T(1,128)S(1)}, u32[]{:S(2)}, u32[]{:S(2)}) async-start(f32[32,21,1,128]{3,2,1,0:T(1,128)} %bitcast.7), calls=%async_computation.1 | async-start | bytes 688128 | tf_op jit(solution)/shard_map/all_to_all | solution.py:416
  30.8 1.6 %copy-start = (f32[32,16384]{1,0:T(8,128)S(1)}, f32[32,16384]{1,0:T(8,128)}, u32[]{:S(2)}) copy-start(f32[32,16384]{1,0:T(8,128)} %param.3) | copy-start | bytes 6291460
  41.1 14.7 %all-to-all-start.2 = ((f32[8,1,128]{2,1,0:T(1,128)}), f32[8,1,128]{2,1,0:T(1,128)S(1)}, u32[]{:S(2)}, u32[]{:S(2)}) async-start(f32[8,1,128]{2,1,0:T(1,128)} %get-tuple-element.13), calls=%async_computation.2 | async-start | bytes 8192 | tf_op jit(solution)/shard_map/all_to_all | solution.py:420

commit v4 on v3

--- a/solution.py
+++ b/solution.py
@@ -1,5 +1,3 @@
-import functools
-
 import jax
 import jax.numpy as jnp
 from jax import lax
@@ -20,8 +18,7 @@
 ANSWER = LOSS + 1
 F32 = jnp.float32
 MIB = 1 << 20
-INNER_MIB, HALVES_MIB, GRADIENT_MIB = 52, 48, 50
-NEAR = 48
+INNER_MIB, GRADIENT_MIB = 52, 52
 WHOLE = pl.BlockSpec(memory_space=pltpu.VMEM)
 FAR = pl.BlockSpec(memory_space=pltpu.HBM)
 
@@ -252,33 +249,62 @@
     )(owner, slabs, target)
 
 
-def halves_kernel(slab, density_in, radiance_in, rim, near, far, density, radiance, held, sems, out_sems):
+def loss_kernel(back, out):
+    total = jnp.sum(back[pl.ds(LOSS, SLABS, stride=ANSWER), :], axis=0, keepdims=True)
+    for z in range(out.shape[0]):
+        out[z] = total
+
+
+def tile_loss(back, count):
+    return call(
+        loss_kernel,
+        "tile_loss",
+        [WHOLE],
+        WHOLE,
+        jax.ShapeDtypeStruct((count, 1, LANES), F32),
+        [],
+        4,
+    )(back)
+
+
+def gradient_kernel(
+    slab, density_in, radiance_in, rim, back, out, density, radiance, held, sems, out_sems
+):
     even = slab[0] % 2 == 0
-    odd_share = jnp.where(even, 0.0, 0.25)
-
-    def one_group(out, first, group, carry):
+
+    def one_group(group, carry):
         base = pl.multiple_of(group * GROUP, GROUP)
+        rows = pl.ds(base, GROUP)
+
+        def answer(q):
+            pair = [
+                back[pl.ds((group * (GROUP // OWNED) + k) * ANSWER + q * OWNED, OWNED), :]
+                for k in range(GROUP // OWNED)
+            ]
+            return jnp.concatenate(pair, axis=0)
+
+        scale = [answer(c) for c in range(3)]
+        left, edge = answer(3), answer(4)
+
+        def seen(colors):
+            return scale[0] * colors[0] + scale[1] * colors[1] + scale[2] * colors[2]
+
+        beside = seen([rim[1 + c, rows, :] for c in range(3)])
+        color = seen([sample_row(radiance, c, 0, base) for c in range(3)])
         here = sample_row(density, 0, 0, base)
-        rows = pl.ds(base, GROUP)
-        color = [sample_row(radiance, c, 0, base) for c in range(3)]
-        beside = [rim[1 + c, rows, :] for c in range(3)]
         before = color
         doubled = jnp.zeros((GROUP, LANES), F32)
         half = None
         for i in range(SAMPLES):
             last = i == SAMPLES - 1
-            after = beside if last else [sample_row(radiance, c, i + 1, base) for c in range(3)]
+            after = beside if last else seen([sample_row(radiance, c, i + 1, base) for c in range(3)])
             if i == 0:
-                new = [0.25 * (color[c] + after[c]) for c in range(3)]
-                store = [new[c] + odd_share * (beside[c] + color[c]) for c in range(3)]
+                new = 0.25 * (color + after)
+                store = new + jnp.where(even, -edge, 0.25 * (beside + color) - left)
             else:
-                transmit = 0.25 * jnp.exp(-0.5 * doubled)
-                new = [half[c] + transmit * (after[c] - before[c]) for c in range(3)]
-                if last:
-                    new = [jnp.where(even, new[c], 0.0) for c in range(3)]
-                store = [half[c] + new[c] for c in range(3)]
-            for c in range(3):
-                out[c * EIGHTS + i // 8, sample_place(i, base - first), :] = store[c]
+                new = half + 0.25 * jnp.exp(-0.5 * doubled) * (after - before)
+                store = half + (jnp.where(even, new - left, -edge) if last else new - left)
+            held[i // 8, sample_place(i, base), :] = store
             if not last:
                 nxt = sample_row(density, 0, i + 1, base)
                 doubled = doubled + (here + nxt)
@@ -287,122 +313,27 @@
         return carry
 
     arrivals = fetches([(density_in, density), (radiance_in, radiance)], sems)
-    departures = fetches([(held, far)], out_sems)
-    start_all(arrivals)
-    each = TILES // GROUP // len(arrivals)
-    kept = NEAR // GROUP // each
-    for k, some in enumerate(arrivals):
-        wait_all([some])
-        out, first = (near, 0) if k < kept else (held, NEAR)
-        lax.fori_loop(k * each, (k + 1) * each, functools.partial(one_group, out, first), 0)
-        if k >= kept:
-            start_all([departures[k - kept]])
-    wait_all(departures)
-
-
-def halves_of(slab, density, radiance, rim, chunks=8):
-    far = (3 * EIGHTS, (TILES - NEAR) * 8, LANES)
-    return call(
-        halves_kernel,
-        "slab_halves",
-        [pl.BlockSpec(memory_space=pltpu.SMEM), FAR, FAR, WHOLE],
-        [WHOLE, FAR],
-        [
-            jax.ShapeDtypeStruct((3 * EIGHTS, NEAR * 8, LANES), F32),
-            jax.ShapeDtypeStruct(far, F32),
-        ],
-        [
-            pltpu.VMEM((EIGHTS, TILES * 8, LANES), F32),
-            pltpu.VMEM((3 * EIGHTS, TILES * 8, LANES), F32),
-            pltpu.VMEM(far, F32),
-            pltpu.SemaphoreType.DMA((chunks, 2)),
-            pltpu.SemaphoreType.DMA((chunks * (TILES - NEAR) // TILES, 1)),
-        ],
-        HALVES_MIB,
-        1_000_000_000,
-    )(slab, density, radiance, rim)
-
-
-def loss_kernel(back, near, out, near_out):
-    total = jnp.sum(back[pl.ds(LOSS, SLABS, stride=ANSWER), :], axis=0, keepdims=True)
-    for z in range(out.shape[0]):
-        out[z] = total
-
-
-def tile_loss(back, near, count):
-    return pl.pallas_call(
-        loss_kernel,
-        in_specs=[WHOLE, WHOLE],
-        out_specs=[WHOLE, WHOLE],
-        out_shape=[
-            jax.ShapeDtypeStruct((count, 1, LANES), F32),
-            jax.ShapeDtypeStruct(near.shape, F32),
-        ],
-        input_output_aliases={1: 1},
-        compiler_params=pltpu.CompilerParams(vmem_limit_bytes=8 * MIB),
-        cost_estimate=pl.CostEstimate(flops=0, bytes_accessed=1024, transcendentals=0),
-        name="tile_loss",
-    )(back, near)
-
-
-def gradient_kernel(slab, near, far_in, back, out, far, held, sems, out_sems):
-    sample = lax.broadcasted_iota(jnp.int32, (8, LANES), 0)
-    even = slab[0] % 2 == 0
-    top = sample == jnp.where(even, 0, 8)
-    bottom = sample == jnp.where(even, 8, 7)
-
-    def one_owner(halves, first, owner, carry):
-        for k in range(OWNED):
-            tile = owner * OWNED + k
-            rows = pl.ds(pl.multiple_of(tile * 8, 8), 8)
-            from_rows = pl.ds(pl.multiple_of((tile - first) * 8, 8), 8)
-            known = [
-                jnp.broadcast_to(back[pl.ds(owner * ANSWER + q * OWNED + k, 1), :], (8, LANES))
-                for q in range(5)
-            ]
-            for a in range(EIGHTS):
-                value = known[0] * halves[a, from_rows, :]
-                value += known[1] * halves[EIGHTS + a, from_rows, :]
-                value += known[2] * halves[2 * EIGHTS + a, from_rows, :]
-                left = known[3]
-                if a == 0:
-                    left = jnp.where(top, known[4], left)
-                if a == EIGHTS - 1:
-                    left = jnp.where(bottom, known[4], left)
-                held[a, rows, :] = value - left
-        return carry
-
-    arrivals = fetches([(far_in, far)], sems)
-    departures = fetches([(held, out)], out_sems)
-    start_all(arrivals)
-    each = SLABS // len(departures)
-    kept = len(departures) - len(arrivals)
-    for k, some in enumerate(departures):
-        if k >= kept:
-            wait_all([arrivals[k - kept]])
-        halves, first = (near, 0) if k < kept else (far, NEAR)
-        lax.fori_loop(k * each, (k + 1) * each, functools.partial(one_owner, halves, first), 0)
-        start_all([some])
-    wait_all(departures)
-
-
-def gradient(slab, near, far, back, chunks=8):
+    in_chunks(arrivals, fetches([(held, out)], out_sems), TILES // GROUP, one_group)
+
+
+def gradient(slab, density, radiance, rim, back, chunks=8):
     shape = (EIGHTS, TILES * 8, LANES)
     return call(
         gradient_kernel,
         "slab_gradient",
-        [pl.BlockSpec(memory_space=pltpu.SMEM), WHOLE, FAR, WHOLE],
+        [pl.BlockSpec(memory_space=pltpu.SMEM), FAR, FAR, WHOLE, WHOLE],
         FAR,
         jax.ShapeDtypeStruct(shape, F32),
         [
-            pltpu.VMEM((3 * EIGHTS, (TILES - NEAR) * 8, LANES), F32),
             pltpu.VMEM(shape, F32),
-            pltpu.SemaphoreType.DMA((chunks * (TILES - NEAR) // TILES, 1)),
+            pltpu.VMEM((3 * EIGHTS, TILES * 8, LANES), F32),
+            pltpu.VMEM(shape, F32),
+            pltpu.SemaphoreType.DMA((chunks, 2)),
             pltpu.SemaphoreType.DMA((chunks, 1)),
         ],
         GRADIENT_MIB,
         1_000_000_000,
-    )(slab, near, far, back)
+    )(slab, density, radiance, rim, back)
 
 
 def on_device(density, radiance, target):
@@ -414,11 +345,10 @@
     answers = scan_slabs(owner, slabs, target)
     answers = answers.reshape(SLABS, ANSWER, 1, LANES)
     back = lax.all_to_all(answers, "depth", 0, 0, tiled=True).reshape(SLABS * ANSWER, LANES)
-    near, far = halves_of(owner, density, radiance, rim)
     zs = lax.axis_size("rays")
-    tile, near = tile_loss(back, near, zs)
+    tile = tile_loss(back, zs)
     losses = lax.all_to_all(tile, "rays", 0, 0, tiled=True)
-    grad = gradient(owner, near, far, back)
+    grad = gradient(owner, density, radiance, rim, back)
     loss_mean = jnp.sum(losses) / (3.0 * zs * TILES * LANES)
     return untiled_view(grad), loss_mean
 

time: 58.5 us -> 57.5 us (0.983)
  blocking collectives: 17.2 us -> 30.4 us
  waiting for transfers between devices: 8.03 us -> 2.76 us
  starting transfers between devices: 15.1 us -> 11.5 us
  Pallas kernels: 13.2 us -> 9.62 us
  local copies, waits for them, and re-layouts: 1.59 us -> 0.01 us
    all_to_all x0 -> x1, blocking collectives: none -> 13.2 us  [on_device(): lax.all_to_all(answers, 'depth', 0, 0, tiled=True)]
    pallas_call x2 -> x1, Pallas kernels: 5.15 us -> 0.6 us  [tile_loss(): call(loss_kernel, 'tile_loss', [WHOLE], WHOLE, jax.ShapeDtypeStruct((coun...]
    all_to_all x1 -> x0, starting transfers between devices: 3.66 us -> none  [on_device(): lax.all_to_all(answers, 'depth', 0, 0, tiled=True)]
    all_to_all x1 -> x0, waiting for transfers between devices: 3.59 us -> none  [on_device(): lax.all_to_all(answers, 'depth', 0, 0, tiled=True)]
    pallas_call x1, Pallas kernels: 3.27 us -> 4.95 us  [gradient(): call(gradient_kernel, 'slab_gradient', [pl.BlockSpec(memory_space=pltpu.S...]
    all_to_all x1, waiting for transfers between devices: 3.28 us -> 1.6 us  [on_device(): losses = lax.all_to_all(tile, 'rays', 0, 0, tiled=True)]
    unnamed x4 -> x2, local copies, waits for them, and re-layouts: 1.59 us -> 0.01 us
    pallas_call x1, Pallas kernels: 0.97 us -> 0.24 us  [scan_slabs(): call(scan_kernel, 'scan_slabs', [pl.BlockSpec(memory_space=pltpu.SMEM), W...]
  transfers between devices with their start and end apart: 3 -> 2, of which waited for: 3 -> 2; matrix products, arithmetic and copies ran while one was open for 0% -> 0% of each run, Pallas kernels for 13% -> 9%
where the time goes in v4:
time: 57.5 us; the launch traced here: 57.3 us
  blocking collectives  30.4 us (53%)
  starting transfers between devices  11.5 us (20%)
  Pallas kernels  9.62 us (17%)
  waiting for transfers between devices  2.76 us (5%)
  between operations  2.44 us (4%)
  other arithmetic  0.61 us (1%)
    all_to_all x1, blocking collectives, on_device(): lax.all_to_all(closing(owner, known, rim), 'depth', 0, 0, tiled=True)  17.2 us
    all_to_all x1, blocking collectives, on_device(): lax.all_to_all(answers, 'depth', 0, 0, tiled=True)  13.2 us
    all_to_all x1, starting transfers between devices, on_device(): losses = lax.all_to_all(tile, 'rays', 0, 0, tiled=True)  8.19 us
    pallas_call x1, Pallas kernels, gradient(): call(gradient_kernel, 'slab_gradient', [pl.BlockSpec(memory_space=pltpu.S...  4.95 us
    pallas_call x1, Pallas kernels, inner(): call(inner_kernel, 'slab_inner', [pl.BlockSpec(memory_space=pltpu.SMEM),...  3.76 us
    ppermute x1, starting transfers between devices, on_device(): rim = lax.ppermute(edge, 'depth', [(s, s ^ 1) for s in range(SLABS)])  3.29 us
    all_to_all x1, waiting for transfers between devices, on_device(): losses = lax.all_to_all(tile, 'rays', 0, 0, tiled=True)  1.6 us
    ppermute x1, waiting for transfers between devices, on_device(): rim = lax.ppermute(edge, 'depth', [(s, s ^ 1) for s in range(SLABS)])  1.16 us
  transfers between devices with their start and end apart: 2, of which 2 were waited for; matrix products, arithmetic and copies ran while one was open for 0% of the time, Pallas kernels for 9%

profile of v4, /device:TPU:1, one launch (start us, length us, event | category | flops | bytes accessed | tf_op | source)
XLA Modules:
  0.0 57.3 jit_solution(10953494535446094686)
XLA Ops:
  0.6 3.8 %slab_inner.1 = (f32[12,128,128]{2,1,0:T(8,128)S(1)}, f32[4,128,128]{2,1,0:T(8,128)S(1)}) custom-call(s32[1]{0:T(128)} %bitcast.slab.owner, f32[4,1024,128]{2,1,0:T(8,128)} %bitcast.23, f32[12,1024,128]{2,1,0:T(8,128)} %bitcast.21), custom_call_target="tpu_custom_call" | custom-call | bytes 1024 | tf_op jit(solution)/shard_map/slab_inner/pallas_call | solution.py:128
  4.4 0.0 copy-start
  4.4 3.3 %collective-permute-start = (f32[4,128,128]{2,1,0:T(8,128)S(1)}, f32[4,128,128]{2,1,0:T(8,128)S(1)}, u32[]{:S(2)}, u32[]{:S(2)}) collective-permute-start(f32[4,128,128]{2,1,0:T(8,128)S(1)} %get-tuple-element.4), channel_id=1, source_target_pairs={{0,8},{8,0},{16,24},{24,16},{32,40},{40,32},{48,56},{56,48},{64,72... | collective-permute-start | bytes 786440 | tf_op jit(solution)/shard_map/ppermute | solution.py:343
  7.7 1.2 %collective-permute-done.rim = f32[4,128,128]{2,1,0:T(8,128)S(1)} collective-permute-done((f32[4,128,128]{2,1,0:T(8,128)S(1)}, f32[4,128,128]{2,1,0:T(8,128)S(1)}, u32[]{:S(2)}, u32[]{:S(2)}) %collective-permute-start) | collective-permute-done | bytes 262176 | tf_op jit(solution)/shard_map/ppermute | solution.py:343
  8.9 0.1 slab_closing.1
  8.9 17.2 %all_to_all.15.slabs = f32[32,32,128]{2,1,0:T(8,128)S(1)} all-to-all(f32[32,32,128]{2,1,0:T(8,128)S(1)} %slab_closing.1), channel_id=1, replica_groups=mesh['depth'=32,'rays'=8] {'depth'}, dimensions={0} | all-to-all | bytes 1048576 | tf_op jit(solution)/shard_map/all_to_all | solution.py:344
  26.1 0.0 copy-done
  26.1 0.2 scan_slabs.1
  26.4 13.2 %all_to_all.16 = f32[32,21,1,128]{3,2,1,0:T(1,128)S(1)} all-to-all(f32[32,21,1,128]{3,2,1,0:T(1,128)S(1)} %bitcast.20), channel_id=1, replica_groups=mesh['depth'=32,'rays'=8] {'depth'}, dimensions={0} | all-to-all | bytes 688128 | tf_op jit(solution)/shard_map/all_to_all | solution.py:347
  39.6 0.6 %tile_loss.1 = f32[8,1,128]{2,1,0:T(1,128)} custom-call(f32[672,128]{1,0:T(8,128)S(1)} %bitcast.18), custom_call_target="tpu_custom_call" | custom-call | bytes 1024 | tf_op jit(solution)/shard_map/tile_loss/pallas_call | solution.py:259
  40.2 8.2 %all-to-all-start.2 = ((f32[8,1,128]{2,1,0:T(1,128)}), f32[8,1,128]{2,1,0:T(1,128)S(1)}, u32[]{:S(2)}, u32[]{:S(2)}) async-start(f32[8,1,128]{2,1,0:T(1,128)} %tile_loss.1), calls=%async_computation.2 | async-start | bytes 8192 | tf_op jit(solution)/shard_map/all_to_all | solution.py:350
  48.4 5.0 %slab_gradient.1 = f32[4,1024,128]{2,1,0:T(8,128)} custom-call(s32[1]{0:T(128)} %bitcast.slab.owner, f32[4,1024,128]{2,1,0:T(8,128)} %bitcast.24, f32[12,1024,128]{2,1,0:T(8,128)} %bitcast.22, f32[4,128,128]{2,1,0:T(8,128)S(1)} %collective-permute-done.rim, f32[672,128]{1,0:T(8,128)S(1)} %bitcast.19), custom_call_target="tpu_custom_call" | custom-call | flops 1000000000 | bytes 1024 | tf_op jit(solution)/shard_map/slab_gradient/pallas_call | solution.py:321
  53.3 1.6 %all-to-all-done.2 = f32[8,1,128]{2,1,0:T(1,128)S(1)} async-done(((f32[8,1,128]{2,1,0:T(1,128)}), f32[8,1,128]{2,1,0:T(1,128)S(1)}, u32[]{:S(2)}, u32[]{:S(2)}) %all-to-all-start.2) | async-done | bytes 4128 | tf_op jit(solution)/shard_map/all_to_all | solution.py:350
  54.9 0.6 %reduce_sum.9 = f32[]{:T(128)} reduce(f32[8,1,128]{2,1,0:T(1,128)S(1)} %all-to-all-done.2, f32[]{:T(128)} %constant.9.clone.1), dimensions={0,1,2}, to_apply=%region_0.0 | reduce | flops 1023 | bytes 4104 | tf_op jit(solution)/shard_map/reduce_sum | solution.py:352
Async XLA Ops:
  4.4 21.7 %copy-start = (f32[3,16384]{1,0:T(4,128)S(1)}, f32[3,16384]{1,0:T(4,128)}, u32[]{:S(2)}) copy-start(f32[3,16384]{1,0:T(4,128)} %target.1) | copy-start | bytes 589828
  4.4 4.5 %collective-permute-start = (f32[4,128,128]{2,1,0:T(8,128)S(1)}, f32[4,128,128]{2,1,0:T(8,128)S(1)}, u32[]{:S(2)}, u32[]{:S(2)}) collective-permute-start(f32[4,128,128]{2,1,0:T(8,128)S(1)} %get-tuple-element.4), channel_id=1, source_target_pairs={{0,8},{8,0},{16,24},{24,16},{32,40},{40,32},{48,56},{56,48},{64,72... | collective-permute-start | bytes 786440 | tf_op jit(solution)/shard_map/ppermute | solution.py:343
  40.2 14.7 %all-to-all-start.2 = ((f32[8,1,128]{2,1,0:T(1,128)}), f32[8,1,128]{2,1,0:T(1,128)S(1)}, u32[]{:S(2)}, u32[]{:S(2)}) async-start(f32[8,1,128]{2,1,0:T(1,128)} %tile_loss.1), calls=%async_computation.2 | async-start | bytes 8192 | tf_op jit(solution)/shard_map/all_to_all | solution.py:350
